TPU v7x, 32 devices: a whole 2x2x4 slice. The times are simulated.
32 devices in a mesh: groups: 2 (over y), seq: 4 (over z), head: 4 (over x, core).
Axes of the slice: x: 2, y: 2, z: 4, core: 2. Of those that a mesh axis runs over, the one named last changes fastest.
Arguments:
- tile_tokens: bfloat16 [16, 256, 1536], P(('groups', 'seq')), parts along dimension 0, may hold values from -6 to 6
- tile_gain: float32 [1536], replicated, may hold values from 0.1 to 1.9
- w_gate_up: bfloat16 [2, 1536, 4096], P(None, 'seq', 'head'), may hold values from -0.15625 to 0.15625
- w_down: bfloat16 [4096, 1536], P('head', 'seq'), may hold values from -0.09375 to 0.09375
- layer_scale: float32 [1536], replicated, may hold values from 1 to 8
- fc_gain: float32 [1536], replicated, may hold values from 0.1 to 1.9
- w_embed: bfloat16 [1536, 768], P(None, 'head'), may hold values from -0.15625 to 0.15625
- embed_bias: float32 [768], P('head'), may hold values from -3 to 3
- pre_emb: bfloat16 [2032, 768], P(('groups', 'seq'), 'head'), parts along dimension 0, may hold values from -6 to 6
- tile_order: int32 [2048], P('groups'), parts along dimension 0, may hold values from 0 to 1023, as said below
- valid_count: int32 [2], P('groups'), parts along dimension 0, may hold values from 256 to 1024
- slide_gain: float32 [768], replicated, may hold values from 0.1 to 1.9
- w_qkv: bfloat16 [3, 768, 768], P(None, None, 'head'), may hold values from -1.25 to 1.25
- sub_gain: float32 [768], P('head'), may hold values from 0.1 to 1.9
- w_out: bfloat16 [768, 768], P('head'), may hold values from -0.21875 to 0.21875
Outputs:
- mixed: float32 [2048, 768], P(('groups', 'seq'), 'head'), parts along dimension 0
There are 2 independent parts, one for each index of `groups`. A program takes and returns all parts, laid end to end along the dimension named above; an argument that names none is the same for every part. Nothing has to cross between parts.
Inputs may be any that keep to these rules, and one draw needn't show every extreme that they name: `tile_order`: A permutation of 0 to 1023. For every block of 256 positions (d * 256 to (d + 1) * 256 - 1) and every block of 256 stored rows, exactly 64 positions of the first take rows of the second.
All inputs are finite; a program needn't handle non-finite values.
Results may differ from a plain program's by a relative error of at most 0.0046.
Values may be sent and summed in bfloat16 or wider, within the bound.
A program may use at most 64 MiB of HBM per device.

v0:
```python
import math

import jax
import jax.numpy as jnp
from jax import lax
from jax.sharding import PartitionSpec as P

DS = 768
HEAD_DIM = 48
SPAN0 = 1024
SPAN1 = 4096
DILATION_SECOND = 4
DILATION_THIRD = 16


layer_eps = 1e-05
masked_score = -1e30


def from_partner(value, axis, bit):
    mask = 2**bit
    pairs = [(source, source ^ mask) for source in range(lax.axis_size(axis))]
    return lax.ppermute(value, axis, pairs)


def normalize(values, gain):
    centered = values - jnp.mean(values, axis=-1, keepdims=True)
    variance = jnp.mean(centered * centered, axis=-1, keepdims=True)
    return centered * lax.rsqrt(variance + layer_eps) * gain


def select_rows(stacked, dilation, offsets):
    group_count, row_count, row_width = stacked.shape
    head_count = offsets.shape[0]
    arranged = stacked.reshape(
        group_count, row_count // dilation, dilation, head_count, row_width // head_count
    )
    choose = jnp.arange(dilation, dtype=jnp.int32)[:, None] == offsets[None, :]
    chosen = jnp.sum(
        jnp.where(choose[None, None, :, :, None], arranged, jnp.zeros((), stacked.dtype)), axis=2
    )
    return chosen.reshape(group_count, row_count // dilation, row_width)


def scatter_rows(attended, log_mass, dilation, offsets):
    query_count, head_count, head_size = attended.shape
    choose = jnp.arange(dilation, dtype=jnp.int32)[:, None] == offsets[None, :]
    spread_out = jnp.where(choose[None, :, :, None], attended[:, None, :, :], 0.0).reshape(
        query_count * dilation, head_count, head_size
    )
    spread_mass = jnp.where(choose[None, :, :], log_mass[:, None, :], masked_score).reshape(
        query_count * dilation, head_count
    )
    selected = jnp.broadcast_to(choose[None, :, :], (query_count, dilation, head_count)).reshape(
        query_count * dilation, head_count
    )
    return (spread_out, spread_mass, selected)


def attend(query_rows, key_rows, value_rows, positions, valid_limit, head_count):
    head_size = query_rows.shape[1] // head_count
    query_heads = query_rows.reshape(query_rows.shape[0], head_count, head_size)
    key_heads = key_rows.reshape(key_rows.shape[0], head_count, head_size)
    value_heads = value_rows.reshape(value_rows.shape[0], head_count, head_size)
    scores = jnp.einsum(
        "qhe,khe->hqk", query_heads, key_heads, preferred_element_type=jnp.float32
    ) / math.sqrt(head_size)
    scores = jnp.where((positions < valid_limit)[:, None, :], scores, masked_score)
    highest = jnp.max(scores, axis=-1, keepdims=True)
    exponent = jnp.exp(scores - highest)
    mass_sum = jnp.sum(exponent, axis=-1, keepdims=True)
    weights = (exponent / mass_sum).astype(jnp.bfloat16)
    attended = jnp.einsum("hqk,khe->qhe", weights, value_heads, preferred_element_type=jnp.float32)
    return (attended, (highest[..., 0] + jnp.log(mass_sum[..., 0])).T)


def body(
    tile_tokens,
    tile_gain,
    w_gate_up,
    w_down,
    layer_scale,
    fc_gain,
    w_embed,
    embed_bias,
    pre_emb,
    tile_order,
    valid_count,
    slide_gain,
    w_qkv,
    sub_gain,
    w_out,
):
    new_count, patch_count, tile_width = tile_tokens.shape
    token_rows = tile_tokens.reshape(new_count * patch_count, tile_width)
    normed = normalize(token_rows.astype(jnp.float32), tile_gain).astype(jnp.bfloat16)
    hidden_width = w_gate_up.shape[2]
    gate_up = jnp.einsum(
        "rk,gkf->grf",
        normed,
        lax.all_gather(w_gate_up, "seq", axis=1, tiled=True),
        preferred_element_type=jnp.float32,
    )
    hidden = (jax.nn.silu(gate_up[0]) * gate_up[1]).astype(jnp.bfloat16)
    pooled_hidden = jnp.mean(
        hidden.reshape(new_count, patch_count, hidden_width), axis=1, dtype=jnp.float32
    )
    everyone = lax.all_gather(pooled_hidden, "seq", axis=0, tiled=True)
    local_part = jnp.dot(everyone, w_down.astype(jnp.float32), precision=lax.Precision.HIGHEST)
    pooled_part = lax.all_to_all(local_part, "seq", split_axis=0, concat_axis=1, tiled=True)
    summed = lax.psum(pooled_part, "head")
    pooled = jnp.mean(tile_tokens, axis=1, dtype=jnp.float32) + layer_scale * summed
    feature = normalize(pooled, fc_gain).astype(jnp.bfloat16)
    new_rows = (jnp.dot(feature, w_embed, preferred_element_type=jnp.float32) + embed_bias).astype(
        jnp.bfloat16
    )
    stored = jnp.concatenate([new_rows, pre_emb], axis=0)
    block_rows = stored.shape[0]
    total_rows = tile_order.shape[0]
    peer_rows = block_rows // lax.axis_size("seq")
    device = lax.axis_index("seq")
    local_index = jnp.arange(block_rows, dtype=jnp.int32)
    inverse = (
        jnp.zeros((total_rows,), jnp.int32)
        .at[tile_order]
        .set(jnp.arange(total_rows, dtype=jnp.int32))
    )
    placed = lax.dynamic_slice_in_dim(inverse, device * block_rows, block_rows)
    target = placed // block_rows
    before = (target[:, None] == target[None, :]) & (placed[None, :] < placed[:, None])
    slot_index = target * peer_rows + jnp.sum(before, axis=1, dtype=jnp.int32)
    routing = (slot_index[None, :] == local_index[:, None]).astype(jnp.bfloat16)
    outgoing = jnp.dot(routing, stored, preferred_element_type=jnp.float32).astype(jnp.bfloat16)
    incoming = lax.all_to_all(outgoing, "seq", split_axis=0, concat_axis=0, tiled=True)
    wanted = lax.dynamic_slice_in_dim(tile_order, device * block_rows, block_rows)
    source = wanted // block_rows
    earlier = (source[:, None] == source[None, :]) & (local_index[None, :] < local_index[:, None])
    arrival = source * peer_rows + jnp.sum(earlier, axis=1, dtype=jnp.int32)
    own_part = jnp.take(incoming, arrival, axis=0)
    sequence = lax.all_gather(own_part, "head", axis=1, tiled=True)
    slide_normed = normalize(sequence.astype(jnp.float32), slide_gain).astype(jnp.bfloat16)
    projected_rows = jnp.einsum(
        "rd,gdc->grc", slide_normed, w_qkv, preferred_element_type=jnp.float32
    ).astype(jnp.bfloat16)
    cols_here = projected_rows.shape[2]
    head_count = cols_here // HEAD_DIM
    head_indices = lax.axis_index("head") * head_count + jnp.arange(head_count, dtype=jnp.int32)
    valid_limit = valid_count[0]
    row_index = device * block_rows + local_index
    near_devices = min(SPAN0, total_rows) // block_rows
    near_rows = projected_rows[1:]
    for bit_index in range(near_devices.bit_length() - 1):
        partner = from_partner(near_rows, "seq", bit_index)
        upper_half = device // (1 << bit_index) % 2 == 1
        near_rows = jnp.where(
            upper_half,
            jnp.concatenate([partner, near_rows], 1),
            jnp.concatenate([near_rows, partner], 1),
        )
    near_start = device // near_devices * near_devices * block_rows
    near_pos = jnp.broadcast_to(
        near_start + jnp.arange(near_rows.shape[1], dtype=jnp.int32),
        (head_count, near_rows.shape[1]),
    )
    near_out, near_mass = attend(
        projected_rows[0], near_rows[0], near_rows[1], near_pos, valid_limit, head_count
    )
    near_sel = jnp.ones((block_rows, head_count), dtype=bool)
    middle_level_offsets = head_indices % DILATION_SECOND
    middle_level = select_rows(projected_rows, DILATION_SECOND, middle_level_offsets)
    middle_devices = min(SPAN1, total_rows) // block_rows
    middle_key_value = middle_level[1:]
    every_row = lax.all_gather(middle_key_value, "seq", axis=1, tiled=True)
    group_rows = middle_devices * middle_key_value.shape[1]
    middle_key_value = lax.dynamic_slice_in_dim(
        every_row, device // middle_devices * group_rows, group_rows, 1
    )
    middle_start = device // middle_devices * middle_devices * block_rows
    middle_pos = (
        middle_start
        + middle_level_offsets[:, None]
        + DILATION_SECOND * jnp.arange(middle_key_value.shape[1], dtype=jnp.int32)[None, :]
    )
    middle_attention, middle_log_sum = attend(
        middle_level[0],
        middle_key_value[0],
        middle_key_value[1],
        middle_pos,
        valid_limit,
        head_count,
    )
    middle_output, middle_level_mass, middle_selected = scatter_rows(
        middle_attention, middle_log_sum, DILATION_SECOND, middle_level_offsets
    )
    distant_offsets = head_indices % DILATION_THIRD
    distant_local_rows = select_rows(projected_rows, DILATION_THIRD, distant_offsets)
    distant_key_value = lax.all_gather(distant_local_rows[1:], "seq", axis=1, tiled=True)
    distant_positions = (
        distant_offsets[:, None]
        + DILATION_THIRD * jnp.arange(distant_key_value.shape[1], dtype=jnp.int32)[None, :]
    )
    distant_attention, distant_log_sum = attend(
        distant_local_rows[0],
        distant_key_value[0],
        distant_key_value[1],
        distant_positions,
        valid_limit,
        head_count,
    )
    distant_output, distant_mass, distant_selected = scatter_rows(
        distant_attention, distant_log_sum, DILATION_THIRD, distant_offsets
    )
    outputs = jnp.stack([near_out, middle_output, distant_output])
    masses = jnp.stack([near_mass, middle_level_mass, distant_mass])
    selects = jnp.stack([near_sel, middle_selected, distant_selected])
    ceiling = jnp.max(masses, axis=0)
    shares = jnp.where(selects, jnp.exp(masses - ceiling), 0.0)
    combined = jnp.sum(shares[..., None] * outputs, axis=0) / jnp.sum(shares, axis=0)[..., None]
    combined = jnp.where((row_index < valid_limit)[:, None, None], combined, 0.0).reshape(
        block_rows, cols_here
    )
    row_total, row_square = lax.psum(
        (jnp.sum(combined, axis=1), jnp.sum(combined * combined, axis=1)), "head"
    )
    mean_value = row_total / DS
    mean_square = row_square / DS
    scaling = lax.rsqrt(mean_square - mean_value * mean_value + layer_eps)
    settled = ((combined - mean_value[:, None]) * scaling[:, None] * sub_gain).astype(jnp.bfloat16)
    partial_rows = jnp.dot(settled, w_out, preferred_element_type=jnp.float32)
    branch_sum = lax.psum_scatter(partial_rows, "head", scatter_dimension=1, tiled=True)
    return own_part.astype(jnp.float32) + branch_sum


def solution(mesh):
    placed = (
        P(("groups", "seq"), None, None),
        P(),
        P(None, "seq", "head"),
        P("head", "seq"),
        P(),
        P(),
        P(None, "head"),
        P("head"),
        P(("groups", "seq"), "head"),
        P("groups"),
        P("groups"),
        P(),
        P(None, None, "head"),
        P("head"),
        P("head", None),
    )
    return jax.shard_map(
        body, mesh=mesh, in_specs=placed, out_specs=P(("groups", "seq"), "head"), check_vma=False
    )
```

profile of v0, /device:TPU:1, one launch (start us, length us, event | category | flops | bytes accessed | tf_op | source)
XLA Modules:
  0.0 280.6 jit_solution(12463239555199441893)
XLA Ops:
  6.6 0.7 all-gather.3.cloned.1.call-update
  7.3 2.0 convert_reduce_fusion.1
  9.3 0.5 multiply_reduce_fusion
  10.5 4.3 %scatter_custom_fusion = s32[1024]{0:T(1024)S(1)} fusion(s32[1024]{0:T(1024)S(1)} %compare_select_fusion, s32[1024]{0:T(1024)S(1)} %iota.73, s32[]{:T(128)} %constant.151.clone.1), kind=kCustom, calls=%fused_computation.103 | custom fusion | bytes 4100 | tf_op jit(solution)/shard_map/scatter | solution.py:126
  15.6 1.7 fusion.4
  17.3 109.2 %all-gather.3.cloned.1.call-done = bf16[2,1536,1024]{2,1,0:T(8,128)(2,1)} async-done(((bf16[2,384,1024]{2,1,0:T(8,128)(2,1)}), bf16[2,1536,1024]{2,1,0:T(8,128)(2,1)}) %all-gather.3.cloned.1.call-update) | async-done | bytes 6291472 | tf_op jit(solution)/shard_map/all_gather | solution.py:101
  126.5 6.0 %convolution_bitcast_fusion = f32[2,512,1024]{2,1,0:T(8,128)S(1)} fusion(bf16[2,1536,1024]{2,1,0:T(8,128)(2,1)} %all-gather.3.cloned.1.call-done, bf16[512,1536]{1,0:T(8,128)(2,1)} %fusion.4), kind=kOutput, calls=%fused_computation.14 | convolution fusion | flops 3221225472 | bytes 12058624 | tf_op jit(solution)/shard_map/rk,gkf->grf/dot_general | solution.py:98
  132.5 0.6 fusion.51
  133.1 0.6 convert_reduce_fusion.2
  133.8 10.3 %all-gather = f32[4,2,1024]{2,1,0:T(2,128)S(1)} all-gather(f32[1,2,1024]{2,1,0:T(2,128)S(1)} %multiply_bitcast_fusion), channel_id=1, replica_groups=mesh['groups'=2,'seq'=4,'head'=4] {'seq'}, dimensions={0}, use_global_device_ids=true | all-gather | bytes 40960 | tf_op jit(solution)/shard_map/all_gather | solution.py:108
  144.5 0.6 all_to_all.22
  145.1 3.3 %all-to-all-start = ((f32[4,2,384]{2,1,0:T(2,128)}), f32[4,2,384]{2,1,0:T(2,128)S(1)}, u32[]{:S(2)}, u32[]{:S(2)}) async-start(f32[4,2,384]{2,1,0:T(2,128)} %all_to_all.22), calls=%async_computation | async-start | bytes 24576 | tf_op jit(solution)/shard_map/all_to_all | solution.py:110
  148.4 4.4 %all-to-all-done = f32[4,2,384]{2,1,0:T(2,128)S(1)} async-done(((f32[4,2,384]{2,1,0:T(2,128)}), f32[4,2,384]{2,1,0:T(2,128)S(1)}, u32[]{:S(2)}, u32[]{:S(2)}) %all-to-all-start) | async-done | bytes 12320 | tf_op jit(solution)/shard_map/all_to_all | solution.py:110
  152.8 13.6 %psum.21 = f32[2,1536]{1,0:T(2,128)S(1)} all-reduce(f32[2,1536]{1,0:T(2,128)S(1)} %bitcast.134), channel_id=1, replica_groups=mesh['groups'=2,'seq'=4,'head'=4] {'head'}, use_global_device_ids=true, to_apply=%region_7.8 | all-reduce | flops 3072 | bytes 24576 | tf_op jit(solution)/shard_map/psum | solution.py:111
  167.4 0.8 copy.71
  168.2 3.3 %all-to-all-start.1 = ((bf16[4,64,192]{2,1,0:T(8,128)(2,1)}), bf16[4,64,192]{2,1,0:T(8,128)(2,1)S(1)}, u32[]{:S(2)}, u32[]{:S(2)}) async-start(bf16[4,64,192]{2,1,0:T(8,128)(2,1)} %bitcast.8), calls=%async_computation.1 | async-start | bytes 262144 | tf_op jit(solution)/shard_map/all_to_all | solution.py:134
  172.3 3.9 %all-to-all-done.1 = bf16[4,64,192]{2,1,0:T(8,128)(2,1)S(1)} async-done(((bf16[4,64,192]{2,1,0:T(8,128)(2,1)}), bf16[4,64,192]{2,1,0:T(8,128)(2,1)S(1)}, u32[]{:S(2)}, u32[]{:S(2)}) %all-to-all-start.1) | async-done | bytes 98336 | tf_op jit(solution)/shard_map/all_to_all | solution.py:134
  176.2 1.2 gather_fusion
  177.5 8.6 %all_gather.17 = bf16[256,768]{0,1:T(8,128)(2,1)S(1)} all-gather(bf16[256,192]{0,1:T(8,128)(2,1)S(1)} %broadcast_select_fusion.2), channel_id=1, replica_groups=mesh['groups'=2,'seq'=4,'head'=4] {'head'}, dimensions={1}, use_global_device_ids=true | all-gather | bytes 491520 | tf_op jit(solution)/shard_map/all_gather | solution.py:140
  187.6 0.7 select_reduce_fusion.1
  188.7 11.2 %all_gather.18 = bf16[2,256,192]{2,0,1:T(2,128)(2,1)S(1)} all-gather(bf16[2,64,192]{2,0,1:T(2,128)(2,1)S(1)} %copy.79), channel_id=1, replica_groups=mesh['groups'=2,'seq'=4,'head'=4] {'seq'}, dimensions={1}, use_global_device_ids=true | all-gather | bytes 245760 | tf_op jit(solution)/shard_map/all_gather | solution.py:173
  201.8 0.6 select_reduce_fusion
  202.5 10.2 %all_gather.19 = bf16[2,64,192]{2,1,0:T(8,128)(2,1)S(1)} all-gather(bf16[2,16,192]{2,1,0:T(8,128)(2,1)S(1)} %slice.61), channel_id=1, replica_groups=mesh['groups'=2,'seq'=4,'head'=4] {'seq'}, dimensions={1}, use_global_device_ids=true | all-gather | bytes 61440 | tf_op jit(solution)/shard_map/all_gather | solution.py:197
  215.0 3.4 %collective-permute-done = bf16[2,256,192]{1,2,0:T(8,128)(2,1)S(1)} collective-permute-done((bf16[2,256,192]{1,2,0:T(8,128)(2,1)S(1)}, bf16[2,256,192]{1,2,0:T(8,128)(2,1)S(1)}, u32[]{:S(2)}, u32[]{:S(2)}) %collective-permute-start) | collective-permute-done | bytes 196640 | tf_op jit(solution)/shard_map/ppermute | solution.py:23
  219.0 11.0 %collective-permute-done.1 = bf16[2,512,192]{1,2,0:T(8,128)(2,1)S(1)} collective-permute-done((bf16[2,512,192]{1,2,0:T(8,128)(2,1)S(1)}, bf16[2,512,192]{1,2,0:T(8,128)(2,1)S(1)}, u32[]{:S(2)}, u32[]{:S(2)}) %collective-permute-start.1) | collective-permute-done | bytes 393248 | tf_op jit(solution)/shard_map/ppermute | solution.py:23
  230.2 0.9 fusion
  231.1 1.0 fusion.1
  232.1 1.2 fusion.8
  233.6 15.0 %all-reduce = (f32[256]{0:T(256)S(1)}, f32[256]{0:T(256)S(1)}) all-reduce(f32[256]{0:T(256)S(1)} %get-tuple-element.8, f32[256]{0:T(256)S(1)} %get-tuple-element.7), channel_id=1, replica_groups=mesh['groups'=2,'seq'=4,'head'=4] {'head'}, use_global_device_ids=true, to_apply=%region_25.26 | all-reduce | flops 512 | bytes 4096 | tf_op jit(solution)/shard_map/psum | solution.py:222
  248.7 1.2 fusion.58
  250.0 22.2 %reduce-scatter.2.cloned.1.call-done = f32[256,192]{0,1:T(8,128)} async-done(((f32[256,768]{0,1:T(8,128)}), f32[256,192]{0,1:T(8,128)}) %reduce-scatter.2.cloned.1.call-update) | async-done | bytes 196624 | tf_op jit(solution)/shard_map/reduce_scatter | solution.py:230
  272.2 1.6 convert_add_fusion
  (135 shorter events, 10.1 us)
Async XLA Ops:
  6.5 179.9 %copy-start = (bf16[3,768,192]{1,2,0:T(8,128)(2,1)S(1)}, bf16[3,768,192]{1,2,0:T(8,128)(2,1)}, u32[]{:S(2)}) copy-start(bf16[3,768,192]{1,2,0:T(8,128)(2,1)} %param.27) | copy-start | bytes 2654212
  6.5 2.7 copy-start.1
  6.5 4.0 %copy-start.7 = (s32[1024]{0:T(1024)S(1)}, s32[1024]{0:T(1024)}, u32[]{:S(2)}) copy-start(s32[1024]{0:T(1024)} %param.24) | copy-start | bytes 12292
  6.5 9.1 %copy-start.5 = (f32[1536]{0:T(1024)S(1)}, f32[1536]{0:T(1024)}, u32[]{:S(2)}) copy-start(f32[1536]{0:T(1024)} %param.16) | copy-start | bytes 18436
  6.5 120.0 %all-gather.3.cloned.1.call-start = ((), (), s32[]{:S(2)}) async-start(), calls=%async_computation.3 | async-start | bytes 7864320 | tf_op jit(solution)/shard_map/all_gather | solution.py:101
  133.1 11.0 %copy-start.3 = (bf16[1024,384]{1,0:T(8,128)(2,1)S(1)}, bf16[1024,384]{1,0:T(8,128)(2,1)}, u32[]{:S(2)}) copy-start(bf16[1024,384]{1,0:T(8,128)(2,1)} %param.18) | copy-start | bytes 2359300
  133.1 33.3 %copy-start.6 = (f32[1536]{0:T(1024)S(1)}, f32[1536]{0:T(1024)}, u32[]{:S(2)}) copy-start(f32[1536]{0:T(1024)} %param.19) | copy-start | bytes 18436
  133.1 33.6 %copy-start.9 = (bf16[1536,192]{0,1:T(8,128)(2,1)S(1)}, bf16[1536,192]{0,1:T(8,128)(2,1)}, u32[]{:S(2)}) copy-start(bf16[1536,192]{0,1:T(8,128)(2,1)} %param.21) | copy-start | bytes 1769476
  133.1 33.6 %copy-start.11 = (f32[1536]{0:T(1024)S(1)}, f32[1536]{0:T(1024)}, u32[]{:S(2)}) copy-start(f32[1536]{0:T(1024)} %param.20) | copy-start | bytes 18436
  133.1 33.6 %copy-start.13 = (f32[192]{0:T(256)S(1)}, f32[192]{0:T(256)}, u32[]{:S(2)}) copy-start(f32[192]{0:T(256)} %param.22) | copy-start | bytes 2308
  133.1 34.0 %copy-start.10 = (bf16[254,192]{0,1:T(8,128)(2,1)S(1)}, bf16[254,192]{0,1:T(8,128)(2,1)}, u32[]{:S(2)}) copy-start(bf16[254,192]{0,1:T(8,128)(2,1)} %param.23) | copy-start | bytes 292612
  133.7 52.7 %copy-start.12 = (f32[768]{0:T(1024)S(1)}, f32[768]{0:T(1024)}, u32[]{:S(2)}) copy-start(f32[768]{0:T(1024)} %param.26) | copy-start | bytes 9220
  145.1 7.7 %all-to-all-start = ((f32[4,2,384]{2,1,0:T(2,128)}), f32[4,2,384]{2,1,0:T(2,128)S(1)}, u32[]{:S(2)}, u32[]{:S(2)}) async-start(f32[4,2,384]{2,1,0:T(2,128)} %all_to_all.22), calls=%async_computation | async-start | bytes 24576 | tf_op jit(solution)/shard_map/all_to_all | solution.py:110
  168.2 8.1 %all-to-all-start.1 = ((bf16[4,64,192]{2,1,0:T(8,128)(2,1)}), bf16[4,64,192]{2,1,0:T(8,128)(2,1)S(1)}, u32[]{:S(2)}, u32[]{:S(2)}) async-start(bf16[4,64,192]{2,1,0:T(8,128)(2,1)} %bitcast.8), calls=%async_computation.1 | async-start | bytes 262144 | tf_op jit(solution)/shard_map/all_to_all | solution.py:134
  171.5 100.6 %reduce-scatter.2.cloned.1.call-start = ((), (), s32[]{:S(2)}) async-start(), calls=%async_computation.4 | async-start | bytes 983040 | tf_op jit(solution)/shard_map/reduce_scatter | solution.py:230
  187.0 13.8 %copy-start.2 = (bf16[3,256,192]{1,2,0:T(8,128)(2,1)}, bf16[3,256,192]{1,2,0:T(8,128)(2,1)S(1)}, u32[]{:S(2)}) copy-start(bf16[3,256,192]{1,2,0:T(8,128)(2,1)S(1)} %convert_bitcast_fusion) | copy-start | bytes 884740
  213.6 4.9 %collective-permute-start = (bf16[2,256,192]{1,2,0:T(8,128)(2,1)S(1)}, bf16[2,256,192]{1,2,0:T(8,128)(2,1)S(1)}, u32[]{:S(2)}, u32[]{:S(2)}) collective-permute-start(bf16[2,256,192]{1,2,0:T(8,128)(2,1)S(1)} %slice.71), channel_id=1, source_target_pairs={{0,4},{4,0},{8,12},{12,8},{1,5},{5,1},{9,13},{13,9},{2,6},{6,2},{1... | collective-permute-start | bytes 589832 | tf_op jit(solution)/shard_map/ppermute | solution.py:23
  214.4 15.8 %slice-start = ((bf16[3,256,192]{1,2,0:T(8,128)(2,1)}), bf16[1,256,192]{1,2,0:T(8,128)(2,1)S(1)}, s32[]{:S(2)}) async-start(bf16[3,256,192]{1,2,0:T(8,128)(2,1)} %copy-done.2), calls=%async_computation.5 | async-start | bytes 196608 | tf_op jit(solution)/shard_map/slice | solution.py:166
  218.5 11.4 %collective-permute-start.1 = (bf16[2,512,192]{1,2,0:T(8,128)(2,1)S(1)}, bf16[2,512,192]{1,2,0:T(8,128)(2,1)S(1)}, u32[]{:S(2)}, u32[]{:S(2)}) collective-permute-start(bf16[2,512,192]{1,2,0:T(8,128)(2,1)S(1)} %maximum_select_fusion.1), channel_id=1, source_target_pairs={{0,8},{4,12},{8,0},{12,4},{1,9},{5,13},{9,1},{13,5},{2,10},{6,14},... | collective-permute-start | bytes 1179656 | tf_op jit(solution)/shard_map/ppermute | solution.py:23
  232.1 16.5 %copy-start.8 = (f32[192]{0:T(256)S(1)}, f32[192]{0:T(256)}, u32[]{:S(2)}) copy-start(f32[192]{0:T(256)} %param.28) | copy-start | bytes 2308
  232.1 16.6 %copy-start.4 = (bf16[192,768]{1,0:T(8,128)(2,1)S(1)}, bf16[192,768]{1,0:T(8,128)(2,1)}, u32[]{:S(2)}) copy-start(bf16[192,768]{1,0:T(8,128)(2,1)} %param.29) | copy-start | bytes 884740
Sparse Core Ops, SparseCore 0:
  8.9 117.5 all-gather.2
  250.1 22.0 reduce-scatter.1
where the time goes:
time: 282 us; the launch traced here: 281 us
  waiting for transfers between devices  155 us (55%)
  blocking collectives  68.9 us (24%)
  between operations  14.7 us (5%)
  local copies, waits for them, and re-layouts  12.1 us (4%)
  matrix products  11.7 us (4%)
  other arithmetic  11.2 us (4%)
  starting transfers between devices  7.08 us (3%)
    all_gather x1, waiting for transfers between devices, body(): lax.all_gather(w_gate_up, 'seq', axis=1, tiled=True)  109 us
    reduce_scatter x1, waiting for transfers between devices, body(): lax.psum_scatter(partial_rows, 'head', scatter_dimension=1, tiled=True)  22.2 us
    psum x1, blocking collectives, body(): lax.psum((jnp.sum(combined, axis=1), jnp.sum(combined * combined, axis=1)...  15 us
    ppermute x2, waiting for transfers between devices, from_partner(): return lax.ppermute(value, axis, pairs)  14.4 us
    psum x1, blocking collectives, body(): summed = lax.psum(pooled_part, 'head')  13.6 us
    all_gather x1, blocking collectives, body(): every_row = lax.all_gather(middle_key_value, 'seq', axis=1, tiled=True)  11.2 us
    all_gather x1, blocking collectives, body(): everyone = lax.all_gather(pooled_hidden, 'seq', axis=0, tiled=True)  10.3 us
    all_gather x1, blocking collectives, body(): lax.all_gather(distant_local_rows[1:], 'seq', axis=1, tiled=True)  10.2 us
  transfers between devices with their start and end apart: 6, of which 6 were waited for; matrix products, arithmetic and copies ran while one was open for 4% of the time, Pallas kernels for 0%

commit v1 on v0

--- a/solution.py
+++ b/solution.py
@@ -1,8 +1,11 @@
+import functools
 import math
 
 import jax
 import jax.numpy as jnp
 from jax import lax
+from jax.experimental import pallas as pl
+from jax.experimental.pallas import tpu as pltpu
 from jax.sharding import PartitionSpec as P
 
 DS = 768
@@ -74,7 +77,7 @@
     return (attended, (highest[..., 0] + jnp.log(mass_sum[..., 0])).T)
 
 
-def body(
+def general_body(
     tile_tokens,
     tile_gain,
     w_gate_up,
@@ -231,6 +234,605 @@
     return own_part.astype(jnp.float32) + branch_sum
 
 
+MESH = pl.DeviceIdType.MESH
+W_CHUNKS = 8
+W_CARRY = 5
+
+
+def remote(src, dst, send_sem, recv_sem, device):
+    return pltpu.make_async_remote_copy(
+        src_ref=src,
+        dst_ref=dst,
+        send_sem=send_sem,
+        recv_sem=recv_sem,
+        device_id=device,
+        device_id_type=MESH,
+    )
+
+
+def encode_kernel(
+    tiles,
+    tok_ref,
+    gain_ref,
+    w_ref,
+    down_ref,
+    scale_ref,
+    fc_ref,
+    embed_ref,
+    bias_ref,
+    pre_ref,
+    wcol_ref,
+    sub_ref,
+    pre_out,
+    new_out,
+    wcol_out,
+    sub_out,
+    wall,
+    normed,
+    acc,
+    pooled,
+    means,
+    parts,
+    send_w,
+    recv_w,
+    send_y,
+    recv_y,
+    send_pre,
+    recv_pre,
+    send_fan,
+    recv_fan,
+    send_aux,
+    recv_aux,
+    send_seq,
+    recv_seq,
+    send_part,
+    recv_part,
+    send_new,
+    recv_new,
+):
+    n = lax.axis_size("seq")
+    heads = lax.axis_size("head")
+    groups = lax.axis_size("groups")
+    z = lax.axis_index("seq")
+    hd = lax.axis_index("head")
+    y = lax.axis_index("groups")
+    rows, width = tok_ref.shape
+    patch = rows // tiles
+    depth = width // n
+    hidden_width = w_ref.shape[2]
+    half = W_CHUNKS // 2
+
+    def seq_peer(k):
+        return lax.rem(z + k, n)
+
+    def seq_source(k):
+        return lax.rem(z + n - k, n)
+
+    def head_peer(k):
+        return lax.rem(hd + k, heads)
+
+    def head_source(k):
+        return lax.rem(hd + heads - k, heads)
+
+    if groups == 2:
+        carry, swap = W_CARRY, W_CHUNKS - W_CARRY
+
+        def chunk(side, i):
+            return side * (W_CHUNKS - 1) + i * (1 - 2 * side)
+
+    else:
+        carry, swap = W_CHUNKS, 0
+
+        def chunk(side, i):
+            return i
+
+    barrier = pltpu.get_barrier_semaphore()
+    count = 0
+    for k in range(n):
+        for j in range(heads):
+            if k or j:
+                pl.semaphore_signal(
+                    barrier,
+                    inc=1,
+                    device_id={"seq": seq_peer(k), "head": head_peer(j)},
+                    device_id_type=MESH,
+                )
+                count += 1
+    if groups == 2:
+        pl.semaphore_signal(barrier, inc=1, device_id={"groups": 1 - y}, device_id_type=MESH)
+        count += 1
+    pl.semaphore_wait(barrier, count)
+
+    pending = []
+
+    def start(copy, cond=None):
+        if cond is None:
+            copy.start()
+        else:
+            pl.when(cond)(copy.start)
+        pending.append((copy, cond))
+
+    for k in range(1, n):
+        start(
+            remote(
+                pre_ref, pre_out.at[z, hd], send_pre.at[k], recv_pre.at[k], {"seq": seq_peer(k)}
+            )
+        )
+    step_right = {"seq": lax.min(z + 1, n - 1)}
+    step_left = {"seq": lax.max(z - 1, 0)}
+    for i in range(carry):
+        c = chunk(y, i)
+        start(
+            remote(w_ref.at[c], wall.at[z, c], send_w.at[0, 0, i], recv_w.at[0, 0, i], step_right),
+            z + 1 < n,
+        )
+        start(
+            remote(w_ref.at[c], wall.at[z, c], send_w.at[1, 0, i], recv_w.at[1, 0, i], step_left),
+            z >= 1,
+        )
+    for k in range(1, heads):
+        start(
+            remote(
+                wcol_ref.at[head_peer(k)],
+                wcol_out.at[hd],
+                send_aux.at[0, k],
+                recv_aux.at[0, k],
+                {"head": head_peer(k)},
+            )
+        )
+        start(
+            remote(
+                sub_ref, sub_out.at[hd], send_aux.at[1, k], recv_aux.at[1, k], {"head": head_peer(k)}
+            )
+        )
+        start(
+            remote(
+                pre_ref,
+                pre_out.at[z, hd],
+                send_fan.at[0, k],
+                recv_fan.at[0, k],
+                {"head": head_peer(k)},
+            )
+        )
+    pre_out[z, hd] = pre_ref[...]
+    wcol_out[hd] = wcol_ref[hd]
+    sub_out[hd] = sub_ref[...]
+
+    block = 64
+    means[z] = jnp.zeros((tiles, width), jnp.float32)
+    for tile in range(tiles):
+
+        def norm_rows(i, total):
+            at = pl.ds(pl.multiple_of(tile * patch + i * block, block), block)
+            values = tok_ref[at, :].astype(jnp.float32)
+            out = normalize(values, gain_ref[...]).astype(jnp.bfloat16)
+            for b in range(n):
+                normed[b, at, :] = out[:, b * depth : (b + 1) * depth]
+            return total + jnp.sum(values, axis=0, keepdims=True)
+
+        total = lax.fori_loop(0, patch // block, norm_rows, jnp.zeros((1, width), jnp.float32))
+        means[z, pl.ds(tile, 1), :] = total / patch
+    for k in range(1, n):
+        start(
+            remote(
+                means.at[z], means.at[z], send_seq.at[0, k], recv_seq.at[0, k], {"seq": seq_peer(k)}
+            )
+        )
+
+    columns = 256
+
+    def multiply(weights, owner, first):
+        @pl.loop(0, hidden_width // columns)
+        def _(t):
+            at = pl.ds(pl.multiple_of(t * columns, columns), columns)
+            for g in range(2):
+                if owner is None:
+                    w = weights[pl.ds(g * half, half), :, at]
+                else:
+                    w = weights[owner, pl.ds(g * half, half), :, at]
+                w = w.reshape(depth, columns)
+                x = normed[z if owner is None else owner]
+                value = jnp.dot(x, w, preferred_element_type=jnp.float32)
+                if first:
+                    acc[g, :, at] = value
+                else:
+                    acc[g, :, at] += value
+
+    multiply(w_ref, None, True)
+
+    def owner_of(side, d):
+        return lax.max(z - d, 0) if side == 0 else lax.min(z + d, n - 1)
+
+    def valid(side, d):
+        return z >= d if side == 0 else z + d < n
+
+    def relay(d):
+        for i in range(carry):
+            c = chunk(y, i)
+            for side in range(2):
+                o = owner_of(side, d)
+                slot = wall.at[o, c]
+                there = valid(side, d)
+                onward = step_right if side == 0 else step_left
+                arrive = remote(
+                    slot, slot, send_w.at[side, d - 1, i], recv_w.at[side, d - 1, i], onward
+                )
+                pl.when(there)(arrive.wait_recv)
+                if d + 1 < n:
+                    goes = (z + 1 < n) if side == 0 else (z >= 1)
+                    start(
+                        remote(slot, slot, send_w.at[side, d, i], recv_w.at[side, d, i], onward),
+                        there & goes,
+                    )
+                if i < swap:
+                    start(
+                        remote(
+                            slot,
+                            slot,
+                            send_y.at[side, d - 1, i],
+                            recv_y.at[side, d - 1, i],
+                            {"groups": 1 - y},
+                        ),
+                        there,
+                    )
+
+    def finish(d):
+        for side in range(2):
+            o = owner_of(side, d)
+
+            @pl.when(valid(side, d))
+            def _():
+                for i in range(swap):
+                    slot = wall.at[o, chunk(1 - y, i)]
+                    remote(
+                        slot,
+                        slot,
+                        send_y.at[side, d - 1, i],
+                        recv_y.at[side, d - 1, i],
+                        {"groups": 1 - y},
+                    ).wait_recv()
+                multiply(wall, o, False)
+
+    def fan_out():
+        for k in range(1, n):
+            slot = pre_out.at[seq_source(k), hd]
+            remote(
+                slot, slot, send_pre.at[k], recv_pre.at[k], {"seq": seq_peer(k)}
+            ).wait_recv()
+            for j in range(1, heads):
+                start(
+                    remote(
+                        slot, slot, send_fan.at[k, j], recv_fan.at[k, j], {"head": head_peer(j)}
+                    )
+                )
+
+    fan_out()
+    for d in range(1, n):
+        relay(d)
+        if d > 1:
+            finish(d - 1)
+    if n > 1:
+        finish(n - 1)
+
+    for tile in range(tiles):
+
+        @pl.loop(0, hidden_width // columns)
+        def _(t):
+            at = pl.ds(pl.multiple_of(t * columns, columns), columns)
+            span = pl.ds(tile * patch, patch)
+            gate = acc[0, span, at]
+            hidden = (gate / (1.0 + jnp.exp(-gate)) * acc[1, span, at]).astype(jnp.bfloat16)
+            pooled[z, pl.ds(tile, 1), at] = (
+                jnp.sum(hidden.astype(jnp.float32), axis=0, keepdims=True) / patch
+            )
+
+    for k in range(1, n):
+        start(
+            remote(
+                pooled.at[z],
+                pooled.at[z],
+                send_seq.at[1, k],
+                recv_seq.at[1, k],
+                {"seq": seq_peer(k)},
+            )
+        )
+    for k in range(1, n):
+        for which, buffer in ((0, means), (1, pooled)):
+            slot = buffer.at[seq_source(k)]
+            remote(
+                slot, slot, send_seq.at[which, k], recv_seq.at[which, k], {"seq": seq_peer(k)}
+            ).wait_recv()
+    everyone = jnp.concatenate([pooled[b] for b in range(n)], axis=0)
+    high = everyone.astype(jnp.bfloat16)
+    rest = everyone - high.astype(jnp.float32)
+    middle = rest.astype(jnp.bfloat16)
+    low = (rest - middle.astype(jnp.float32)).astype(jnp.bfloat16)
+    local_part = jnp.zeros((n * tiles, down_ref.shape[1]), jnp.float32)
+    for piece in (low, middle, high):
+        local_part += jnp.dot(piece, down_ref[...], preferred_element_type=jnp.float32)
+    parts[z, hd] = local_part
+    for k in range(n):
+        for j in range(heads):
+            if k or j:
+                start(
+                    remote(
+                        parts.at[z, hd],
+                        parts.at[z, hd],
+                        send_part.at[k, j],
+                        recv_part.at[k, j],
+                        {"seq": seq_peer(k), "head": head_peer(j)},
+                    )
+                )
+    for k in range(n):
+        for j in range(heads):
+            if k or j:
+                slot = parts.at[seq_source(k), head_source(j)]
+                remote(
+                    slot,
+                    slot,
+                    send_part.at[k, j],
+                    recv_part.at[k, j],
+                    {"seq": seq_peer(k), "head": head_peer(j)},
+                ).wait_recv()
+    summed = jnp.concatenate(
+        [sum(parts[b, j] for j in range(heads)) for b in range(n)], axis=1
+    )
+    average = jnp.concatenate([means[b] for b in range(n)], axis=0)
+    feature = normalize(average + scale_ref[...] * summed, fc_ref[...]).astype(jnp.bfloat16)
+    fresh = jnp.dot(feature, embed_ref[...], preferred_element_type=jnp.float32) + bias_ref[...]
+    new_out[hd] = fresh
+    for k in range(1, heads):
+        start(
+            remote(
+                new_out.at[hd], new_out.at[hd], send_new.at[k], recv_new.at[k], {"head": head_peer(k)}
+            )
+        )
+    for k in range(1, heads):
+        peer = {"head": head_peer(k)}
+        source = head_source(k)
+        for slot, sends, receives in (
+            (new_out.at[source], send_new.at[k], recv_new.at[k]),
+            (wcol_out.at[source], send_aux.at[0, k], recv_aux.at[0, k]),
+            (sub_out.at[source], send_aux.at[1, k], recv_aux.at[1, k]),
+        ):
+            remote(slot, slot, sends, receives, peer).wait_recv()
+        for b in range(n):
+            slot = pre_out.at[seq_source(b), source]
+            remote(slot, slot, send_fan.at[b, k], recv_fan.at[b, k], peer).wait_recv()
+    for copy, cond in pending:
+        if cond is None:
+            copy.wait_send()
+        else:
+            pl.when(cond)(copy.wait_send)
+
+
+def encode(
+    tile_tokens,
+    tile_gain,
+    w_gate_up,
+    w_down,
+    layer_scale,
+    fc_gain,
+    w_embed,
+    embed_bias,
+    pre_emb,
+    w_cols,
+    sub_gain,
+):
+    n = lax.axis_size("seq")
+    heads = lax.axis_size("head")
+    tiles, patch, width = tile_tokens.shape
+    depth, hidden_width = w_gate_up.shape[1:]
+    rows = tiles * patch
+    cols = w_embed.shape[1]
+    vmem = pl.BlockSpec(memory_space=pltpu.VMEM)
+    dma = pltpu.SemaphoreType.DMA
+    hops = max(n - 1, 1)
+    return pl.pallas_call(
+        functools.partial(encode_kernel, tiles),
+        out_shape=(
+            jax.ShapeDtypeStruct((n, heads) + pre_emb.shape, jnp.bfloat16),
+            jax.ShapeDtypeStruct((heads, n * tiles, cols), jnp.float32),
+            jax.ShapeDtypeStruct(w_cols.shape, jnp.bfloat16),
+            jax.ShapeDtypeStruct((heads, 1, cols), jnp.float32),
+        ),
+        in_specs=[vmem] * 11,
+        out_specs=(vmem,) * 4,
+        scratch_shapes=[
+            pltpu.VMEM((n, W_CHUNKS, 2 * depth // W_CHUNKS, hidden_width), jnp.bfloat16),
+            pltpu.VMEM((n, rows, depth), jnp.bfloat16),
+            pltpu.VMEM((2, rows, hidden_width), jnp.float32),
+            pltpu.VMEM((n, tiles, hidden_width), jnp.float32),
+            pltpu.VMEM((n, tiles, width), jnp.float32),
+            pltpu.VMEM((n, heads, n * tiles, w_down.shape[1]), jnp.float32),
+            dma((2, hops, W_CHUNKS)),
+            dma((2, hops, W_CHUNKS)),
+            dma((2, hops, W_CHUNKS)),
+            dma((2, hops, W_CHUNKS)),
+            dma((n,)),
+            dma((n,)),
+            dma((n, heads)),
+            dma((n, heads)),
+            dma((2, heads)),
+            dma((2, heads)),
+            dma((2, n)),
+            dma((2, n)),
+            dma((n, heads)),
+            dma((n, heads)),
+            dma((heads,)),
+            dma((heads,)),
+        ],
+        compiler_params=pltpu.CompilerParams(
+            collective_id=0, has_side_effects=True, vmem_limit_bytes=48 * 1024 * 1024
+        ),
+    )(
+        tile_tokens.reshape(rows, width),
+        tile_gain.reshape(1, width),
+        w_gate_up.reshape(W_CHUNKS, 2 * depth // W_CHUNKS, hidden_width),
+        w_down,
+        layer_scale.reshape(1, width),
+        fc_gain.reshape(1, width),
+        w_embed,
+        embed_bias.reshape(1, cols),
+        pre_emb,
+        w_cols,
+        sub_gain.reshape(1, cols),
+    )
+
+
+def settle_kernel(comb_ref, wcol_ref, sub_ref, out_ref, slots, send_sem, recv_sem):
+    heads = lax.axis_size("head")
+    hd = lax.axis_index("head")
+    barrier = pltpu.get_barrier_semaphore()
+    for k in range(1, heads):
+        pl.semaphore_signal(
+            barrier, inc=1, device_id={"head": lax.rem(hd + k, heads)}, device_id_type=MESH
+        )
+    pl.semaphore_wait(barrier, heads - 1)
+    copies = []
+    for k in range(1, heads):
+        copies.append(
+            remote(
+                comb_ref,
+                slots.at[hd],
+                send_sem.at[k],
+                recv_sem.at[k],
+                {"head": lax.rem(hd + k, heads)},
+            )
+        )
+        copies[-1].start()
+    slots[hd] = comb_ref[...]
+    for k in range(1, heads):
+        slot = slots.at[lax.rem(hd + heads - k, heads)]
+        remote(
+            slot, slot, send_sem.at[k], recv_sem.at[k], {"head": lax.rem(hd + k, heads)}
+        ).wait_recv()
+    pieces = [slots[j].astype(jnp.float32) for j in range(heads)]
+    features = heads * pieces[0].shape[1]
+    mean = sum(jnp.sum(p, axis=1, keepdims=True) for p in pieces) / features
+    square = sum(jnp.sum(p * p, axis=1, keepdims=True) for p in pieces) / features
+    scaling = lax.rsqrt(square - mean * mean + layer_eps)
+    total = jnp.zeros(out_ref.shape, jnp.float32)
+    for j in range(heads):
+        settled = ((pieces[j] - mean) * scaling * sub_ref[j]).astype(jnp.bfloat16)
+        total += jnp.dot(settled, wcol_ref[j], preferred_element_type=jnp.float32)
+    out_ref[...] = total
+    for copy in copies:
+        copy.wait_send()
+
+
+def settle(combined, w_cols, sub_all):
+    heads = lax.axis_size("head")
+    vmem = pl.BlockSpec(memory_space=pltpu.VMEM)
+    return pl.pallas_call(
+        settle_kernel,
+        out_shape=jax.ShapeDtypeStruct((combined.shape[0], w_cols.shape[2]), jnp.float32),
+        in_specs=[vmem] * 3,
+        out_specs=vmem,
+        scratch_shapes=[
+            pltpu.VMEM((heads,) + combined.shape, jnp.bfloat16),
+            pltpu.SemaphoreType.DMA((heads,)),
+            pltpu.SemaphoreType.DMA((heads,)),
+        ],
+        compiler_params=pltpu.CompilerParams(collective_id=1, has_side_effects=True),
+    )(combined, w_cols, sub_all)
+
+
+def near_body(
+    tile_tokens,
+    tile_gain,
+    w_gate_up,
+    w_down,
+    layer_scale,
+    fc_gain,
+    w_embed,
+    embed_bias,
+    pre_emb,
+    tile_order,
+    valid_count,
+    slide_gain,
+    w_qkv,
+    sub_gain,
+    w_out,
+):
+    n = lax.axis_size("seq")
+    heads = lax.axis_size("head")
+    device = lax.axis_index("seq")
+    column = lax.axis_index("head")
+    cols = w_embed.shape[1]
+    w_cols = w_out.reshape(cols, heads, cols).transpose(1, 0, 2)
+    pre_all, new_all, w_cols, sub_all = encode(
+        tile_tokens,
+        tile_gain,
+        w_gate_up,
+        w_down,
+        layer_scale,
+        fc_gain,
+        w_embed,
+        embed_bias,
+        pre_emb,
+        w_cols,
+        sub_gain,
+    )
+    total_rows = tile_order.shape[0]
+    block_rows = total_rows // n
+    new_rows = new_all.astype(jnp.bfloat16).transpose(1, 0, 2).reshape(n, -1, heads * cols)
+    old_rows = pre_all.transpose(0, 2, 1, 3).reshape(n, -1, heads * cols)
+    stored = jnp.concatenate([new_rows, old_rows], axis=1).reshape(total_rows, heads * cols)
+    every = jnp.arange(total_rows, dtype=jnp.int32)
+    routing = (tile_order[:, None] == every[None, :]).astype(jnp.bfloat16)
+    sequence = jnp.dot(routing, stored, preferred_element_type=jnp.float32)
+    slide_normed = normalize(sequence, slide_gain).astype(jnp.bfloat16)
+    key_value = jnp.einsum(
+        "rd,gdc->grc", slide_normed, w_qkv[1:], preferred_element_type=jnp.float32
+    ).astype(jnp.bfloat16)
+    own_normed = lax.dynamic_slice_in_dim(slide_normed, device * block_rows, block_rows)
+    query = jnp.dot(own_normed, w_qkv[0], preferred_element_type=jnp.float32).astype(jnp.bfloat16)
+    own_part = lax.dynamic_slice(
+        sequence, (device * block_rows, column * cols), (block_rows, cols)
+    )
+    head_count = cols // HEAD_DIM
+    head_indices = column * head_count + jnp.arange(head_count, dtype=jnp.int32)
+    valid_limit = valid_count[0]
+    row_index = device * block_rows + jnp.arange(block_rows, dtype=jnp.int32)
+    levels = []
+    for dilation in (1, DILATION_SECOND, DILATION_THIRD):
+        if dilation == 1:
+            positions = jnp.broadcast_to(every, (head_count, total_rows))
+            out, mass = attend(
+                query, key_value[0], key_value[1], positions, valid_limit, head_count
+            )
+            levels.append((out, mass, jnp.ones((block_rows, head_count), dtype=bool)))
+            continue
+        offsets = head_indices % dilation
+        chosen_query = select_rows(query[None], dilation, offsets)[0]
+        chosen = select_rows(key_value, dilation, offsets)
+        positions = (
+            offsets[:, None]
+            + dilation * jnp.arange(total_rows // dilation, dtype=jnp.int32)[None, :]
+        )
+        out, mass = attend(
+            chosen_query, chosen[0], chosen[1], positions, valid_limit, head_count
+        )
+        levels.append(scatter_rows(out, mass, dilation, offsets))
+    outputs, masses, selects = (jnp.stack(parts) for parts in zip(*levels))
+    ceiling = jnp.max(masses, axis=0)
+    shares = jnp.where(selects, jnp.exp(masses - ceiling), 0.0)
+    combined = jnp.sum(shares[..., None] * outputs, axis=0) / jnp.sum(shares, axis=0)[..., None]
+    combined = jnp.where((row_index < valid_limit)[:, None, None], combined, 0.0).reshape(
+        block_rows, cols
+    )
+    branch = settle(combined.astype(jnp.bfloat16), w_cols, sub_all)
+    return own_part + branch
+
+
+def body(*args):
+    total_rows = args[9].shape[0]
+    if total_rows <= SPAN0:
+        return near_body(*args)
+    return general_body(*args)
+
+
 def solution(mesh):
     placed = (
         P(("groups", "seq"), None, None),

time: 282 us -> 166 us (0.59)
  waiting for transfers between devices: 155 us -> 0 us
  Pallas kernels: 0 us -> 111 us
  blocking collectives: 68.9 us -> 0 us
  local copies, waits for them, and re-layouts: 12.1 us -> 29.1 us
  between operations: 14.7 us -> 1.45 us
  starting transfers between devices: 7.08 us -> 0 us
  other arithmetic: 11.2 us -> 16.9 us
  matrix products: 11.7 us -> 6.78 us
    pallas_call x0 -> x2, Pallas kernels: none -> 111 us  [the longest x1 100 us: encode(): pl.pallas_call(functools.partial(encode_kernel, tiles), out_shape=(jax.Sh...]
    all_gather x1 -> x0, waiting for transfers between devices: 109 us -> none  [body(): lax.all_gather(w_gate_up, 'seq', axis=1, tiled=True)]
    all_gather x4 -> x0, blocking collectives: 40.3 us -> none  [the longest x1 11.2 us: body(): every_row = lax.all_gather(middle_key_value, 'seq', axis=1, tiled=True)]
    psum x2 -> x0, blocking collectives: 28.6 us -> none  [the longest x1 15 us: body(): lax.psum((jnp.sum(combined, axis=1), jnp.sum(combined * combined, axis=1)...]
    reduce_scatter x1 -> x0, waiting for transfers between devices: 22.2 us -> none  [body(): lax.psum_scatter(partial_rows, 'head', scatter_dimension=1, tiled=True)]
    ppermute x2 -> x0, waiting for transfers between devices: 14.4 us -> none  [from_partner(): return lax.ppermute(value, axis, pairs)]
    unnamed x32 -> x67, local copies, waits for them, and re-layouts: 0.21 us -> 10.3 us
    all_to_all x2 -> x0, waiting for transfers between devices: 8.34 us -> none  [the longest x1 4.4 us: body(): lax.all_to_all(local_part, 'seq', split_axis=0, concat_axis=1, tiled=True)]
  transfers between devices with their start and end apart: 6 -> 0, of which waited for: 6 -> 0; matrix products, arithmetic and copies ran while one was open for 4% -> 0% of each run, Pallas kernels for 0% -> 0%
where the time goes in v1:
time: 166 us; the launch traced here: 165 us
  Pallas kernels  111 us (67%)
  local copies, waits for them, and re-layouts  29.1 us (18%)
  other arithmetic  16.9 us (10%)
  matrix products  6.78 us (4%)
    pallas_call x1, Pallas kernels, encode(): pl.pallas_call(functools.partial(encode_kernel, tiles), out_shape=(jax.Sh...  100 us
    pallas_call x1, Pallas kernels, settle(): pl.pallas_call(settle_kernel, out_shape=jax.ShapeDtypeStruct((combined.sh...  10.7 us
    unnamed x67, local copies, waits for them, and re-layouts  10.3 us
    reduce_sum x4, other arithmetic, select_rows(): jnp.sum(jnp.where(choose[None, None, :, :, None], arranged, jnp.zeros((),...  6.27 us

profile of v1, /device:TPU:1, one launch (start us, length us, event | category | flops | bytes accessed | tf_op | source)
XLA Modules:
  0.0 165.3 jit_solution(4286379307301650970)
XLA Ops:
  5.4 1.3 reshape.479.fc_ref
  8.0 0.7 broadcast_in_dim.271
  8.7 0.7 stack.19
  9.4 1.7 copy.63.pre_ref
  11.1 1.3 reshape.481
  12.5 1.3 copy.62.embed_ref
  13.9 1.4 copy-done.1
  15.3 0.9 copy-done.3
  18.2 100.4 %shard_map.145 = (bf16[4,4,254,192]{3,2,1,0:T(8,128)(2,1)}, f32[4,8,192]{2,1,0:T(8,128)S(1)}, bf16[4,192,192]{2,1,0:T(8,128)(2,1)S(1)}, f32[4,1,192]{2,1,0:T(1,128)S(1)}) custom-call(bf16[512,1536]{1,0:T(8,128)(2,1)S(1)} %bitcast.91, f32[1,1536]{1,0:T(1,128)S(1)} %reshape.476.gain_ref, bf16[8,96,1024]{2,1,0:T(8,128)(2,1)S(1)} %bitcast.92, ...), custom_call_target="tpu_custom_call" | custom-call | tf_op jit(solution)/shard_map/pallas_call | solution.py:631
  118.6 0.7 copy-done.4
  120.0 2.8 %copy.65 = bf16[4,254,4,192]{1,3,2,0:T(8,128)(2,1)S(1)} copy(bf16[4,254,4,192]{3,1,2,0:T(8,128)(2,1)} %bitcast.96) | data formatting | bytes 3121152 | tf_op jit(solution)/shard_map/transpose | solution.py:780
  122.8 1.2 copy.66
  124.0 1.9 %pad_maximum_fusion = bf16[4,256,768]{1,2,0:T(8,128)(2,1)S(1)} fusion(bf16[4,254,768]{1,2,0:T(8,128)(2,1)S(1)} %bitcast.95, bf16[4,2,768]{1,2,0:T(8,128)(2,1)} %copy.66), kind=kLoop, calls=%fused_computation.13 | loop fusion | flops 3145728 | bytes 3145728 | tf_op jit(solution)/shard_map/concatenate | solution.py:781
  125.9 0.7 copy.67
  126.6 2.1 %fusion.34 = (f32[1024]{0:T(1024)S(1)}, f32[1024,768]{0,1:T(8,128)S(1)}) fusion(bf16[1024,768]{1,0:T(8,128)(2,1)S(1)} %bitcast.99, s32[1024]{0:T(1024)S(1)} %copy-done.29), kind=kOutput, calls=%fused_computation.84 | convolution fusion | flops 1612446720 | bytes 4726784 | tf_op jit(solution)/shard_map/dot_general | solution.py:784
  129.8 0.8 copy.88
  130.9 0.8 fusion.37
  132.6 0.9 select_reduce_fusion.3
  133.5 0.8 fusion.31
  134.8 1.1 reshape.488
  135.9 2.5 %select_reduce_fusion = bf16[2,64,4,48]{3,2,1,0:T(4,128)(2,1)S(1)} fusion(bf16[2,64,16,4,48]{4,3,2,1,0:T(4,128)(2,1)S(1)} %reshape.488, pred[16,4]{1,0:T(8,128)(4,1)} %copy-done.16), kind=kLoop, calls=%fused_computation.9 | loop fusion | flops 761856 | bytes 835648 | tf_op jit(solution)/shard_map/reduce_sum | solution.py:42
  138.5 0.9 fusion.35
  141.0 1.3 broadcast_select_fusion
  142.4 1.3 reshape.487
  143.7 2.6 %select_reduce_fusion.1 = bf16[2,256,4,48]{3,2,1,0:T(4,128)(2,1)S(1)} fusion(bf16[2,256,4,4,48]{4,3,2,1,0:T(4,128)(2,1)S(1)} %reshape.487, pred[4,4]{1,0:T(4,128)(4,1)} %copy-done.25), kind=kLoop, calls=%fused_computation.10 | loop fusion | flops 688128 | bytes 983056 | tf_op jit(solution)/shard_map/reduce_sum | solution.py:42
  148.4 0.9 fusion.1
  149.3 1.0 fusion.2
  150.4 1.2 fusion.6
  152.0 0.8 select_convert_fusion.comb_ref
  152.8 10.7 %shard_map.146 = f32[256,192]{1,0:T(8,128)} custom-call(bf16[256,192]{1,0:T(8,128)(2,1)} %select_convert_fusion.comb_ref, bf16[4,192,192]{2,1,0:T(8,128)(2,1)} %copy-done.4, f32[4,1,192]{2,1,0:T(1,128)} %copy-done.6), custom_call_target="tpu_custom_call" | custom-call | tf_op jit(solution)/shard_map/pallas_call | solution.py:727
  163.5 1.0 add.154
  164.5 0.8 copy.86
  (126 shorter events, 15.4 us)
Async XLA Ops:
  0.0 13.8 %copy-start.2 = (bf16[1024,384]{1,0:T(8,128)(2,1)S(1)}, bf16[1024,384]{1,0:T(8,128)(2,1)}, u32[]{:S(2)}) copy-start(bf16[1024,384]{1,0:T(8,128)(2,1)} %down_ref.1) | copy-start | bytes 2359300
  0.0 13.8 %copy-start = (bf16[2,256,1536]{2,1,0:T(8,128)(2,1)S(1)}, bf16[2,256,1536]{2,1,0:T(8,128)(2,1)}, u32[]{:S(2)}) copy-start(bf16[2,256,1536]{2,1,0:T(8,128)(2,1)} %param.15) | copy-start | bytes 4718596
  2.6 0.7 copy-start.25
  3.9 1.5 copy-start.16
  13.8 1.4 copy-start.1
  15.3 0.9 copy-start.3
  16.2 0.7 copy-start.5
  16.9 0.7 copy-start.7
  17.5 0.7 copy-start.8
  118.6 0.8 copy-start.4
  119.3 0.6 copy-start.6
  124.0 2.6 %copy-start.29 = (s32[1024]{0:T(1024)S(1)}, s32[1024]{0:T(1024)}, u32[]{:S(2)}) copy-start(s32[1024]{0:T(1024)} %param.24) | copy-start | bytes 12292
  128.7 0.7 copy-start.24
  129.1 1.5 copy-start.11
  129.1 1.8 %slice-start = ((bf16[3,768,192]{1,2,0:T(8,128)(2,1)}), bf16[2,768,192]{1,2,0:T(8,128)(2,1)S(1)}, s32[]{:S(2)}) async-start(bf16[3,768,192]{1,2,0:T(8,128)(2,1)} %param.27), calls=%async_computation | async-start | bytes 1179648 | tf_op jit(solution)/shard_map/slice | solution.py:787
  130.9 0.9 copy-start.13
  130.9 1.2 copy-start.17
  130.9 1.6 copy-start.26
  142.4 4.5 %copy-start.23 = (pred[4,256]{1,0:T(4,128)(4,1)S(1)}, pred[4,256]{1,0:T(4,128)(4,1)}, u32[]{:S(2)}) copy-start(pred[4,256]{1,0:T(4,128)(4,1)} %add_compare_fusion) | copy-start | bytes 3076
  143.7 3.2 %copy-start.15 = (bf16[64,4,48]{2,1,0:T(4,128)(2,1)S(1)}, bf16[64,4,48]{2,1,0:T(4,128)(2,1)}, u32[]{:S(2)}) copy-start(bf16[64,4,48]{2,1,0:T(4,128)(2,1)} %select_reduce_fusion.3) | copy-start | bytes 73732
  143.7 4.4 %copy-start.21 = (pred[1,256,4]{1,2,0:T(4,128)(4,1)S(1)}, pred[1,256,4]{1,2,0:T(4,128)(4,1)}, u32[]{:S(2)}) copy-start(pred[1,256,4]{1,2,0:T(4,128)(4,1)} %stack.19) | copy-start | bytes 3076
  146.3 2.1 %copy-start.19 = (pred[256,4]{0,1:T(4,128)(4,1)S(1)}, pred[256,4]{0,1:T(4,128)(4,1)}, u32[]{:S(2)}) copy-start(pred[256,4]{0,1:T(4,128)(4,1)} %broadcast_in_dim.271) | copy-start | bytes 3076
  146.3 2.1 %copy-start.14 = (bf16[256,192]{0,1:T(8,128)(2,1)S(1)}, bf16[256,192]{0,1:T(8,128)(2,1)}, u32[]{:S(2)}) copy-start(bf16[256,192]{0,1:T(8,128)(2,1)} %copy-done.13) | copy-start | bytes 294916
  146.3 2.1 %copy-start.22 = (pred[1024]{0:T(1024)(128)(4,1)S(1)}, pred[1024]{0:T(1024)(128)(4,1)}, u32[]{:S(2)}) copy-start(pred[1024]{0:T(1024)(128)(4,1)} %iota_compare_fusion.3) | copy-start | bytes 3076
  149.3 1.0 copy-start.12
  150.3 1.3 copy-start.18
  150.3 1.3 copy-start.20
  150.4 1.3 copy-start.28
  150.4 1.4 copy-start.10
  150.4 1.6 copy-start.27
  150.4 13.1 %copy-start.9 = (f32[256,192]{1,0:T(8,128)S(1)}, f32[256,192]{1,0:T(8,128)}, u32[]{:S(2)}) copy-start(f32[256,192]{1,0:T(8,128)} %copy.88) | copy-start | bytes 589828

commit v2 on v1

--- a/solution.py
+++ b/solution.py
@@ -236,7 +236,7 @@
 
 MESH = pl.DeviceIdType.MESH
 W_CHUNKS = 8
-W_CARRY = 5
+W_CARRY = 4
 
 
 def remote(src, dst, send_sem, recv_sem, device):
@@ -252,21 +252,40 @@
 
 def encode_kernel(
     tiles,
-    tok_ref,
-    gain_ref,
+    valid_ref,
+    tok_hbm,
+    wide_ref,
     w_ref,
-    down_ref,
-    scale_ref,
-    fc_ref,
-    embed_ref,
-    bias_ref,
+    down_hbm,
+    embed_hbm,
     pre_ref,
     wcol_ref,
-    sub_ref,
+    narrow_ref,
+    order_ref,
+    slide_ref,
+    qkv_hbm,
+    out_ref,
+    tok_ref,
+    down_ref,
+    embed_ref,
+    qkv_ref,
     pre_out,
     new_out,
     wcol_out,
     sub_out,
+    seq_rows,
+    projected,
+    fresh_pick,
+    fresh_rows,
+    own_query,
+    mid_out,
+    mid_mass,
+    far_out,
+    far_mass,
+    slots,
+    local_sem,
+    send_mix,
+    recv_mix,
     wall,
     normed,
     acc,
@@ -326,6 +345,19 @@
         def chunk(side, i):
             return i
 
+    loads = [
+        pltpu.make_async_copy(source, target, local_sem.at[i])
+        for i, (source, target) in enumerate(
+            (
+                (tok_hbm, tok_ref),
+                (qkv_hbm, qkv_ref),
+                (down_hbm, down_ref),
+                (embed_hbm, embed_ref),
+            )
+        )
+    ]
+    for load in loads:
+        load.start()
     barrier = pltpu.get_barrier_semaphore()
     count = 0
     for k in range(n):
@@ -382,7 +414,7 @@
         )
         start(
             remote(
-                sub_ref, sub_out.at[hd], send_aux.at[1, k], recv_aux.at[1, k], {"head": head_peer(k)}
+                narrow_ref, sub_out.at[hd], send_aux.at[1, k], recv_aux.at[1, k], {"head": head_peer(k)}
             )
         )
         start(
@@ -396,8 +428,9 @@
         )
     pre_out[z, hd] = pre_ref[...]
     wcol_out[hd] = wcol_ref[hd]
-    sub_out[hd] = sub_ref[...]
-
+    sub_out[hd] = narrow_ref[...]
+
+    loads[0].wait()
     block = 64
     means[z] = jnp.zeros((tiles, width), jnp.float32)
     for tile in range(tiles):
@@ -405,7 +438,7 @@
         def norm_rows(i, total):
             at = pl.ds(pl.multiple_of(tile * patch + i * block, block), block)
             values = tok_ref[at, :].astype(jnp.float32)
-            out = normalize(values, gain_ref[...]).astype(jnp.bfloat16)
+            out = normalize(values, wide_ref[pl.ds(0, 1), :]).astype(jnp.bfloat16)
             for b in range(n):
                 normed[b, at, :] = out[:, b * depth : (b + 1) * depth]
             return total + jnp.sum(values, axis=0, keepdims=True)
@@ -507,10 +540,76 @@
                 )
 
     fan_out()
+    total_rows = order_ref.shape[0]
+    stored_rows = pre_ref.shape[0]
+    cols = pre_ref.shape[1]
+    classes = DILATION_THIRD
+    class_rows = total_rows // classes
+    own_rows = stored_rows // classes
+
+    def row_norm(pieces):
+        features = heads * cols
+        mean = sum(jnp.sum(p, axis=1, keepdims=True) for p in pieces) / features
+        centered = [p - mean for p in pieces]
+        variance = sum(jnp.sum(p * p, axis=1, keepdims=True) for p in centered) / features
+        scaling = lax.rsqrt(variance + layer_eps)
+        return [
+            (p * scaling * slide_ref[pl.ds(j, 1), :]).astype(jnp.bfloat16)
+            for j, p in enumerate(centered)
+        ]
+
+    def project(pieces, g):
+        return sum(
+            jnp.dot(
+                piece,
+                qkv_ref[g, j * cols : (j + 1) * cols, :],
+                preferred_element_type=jnp.float32,
+            )
+            for j, piece in enumerate(pieces)
+        )
+
+    def stored_sequence():
+        for k in range(1, heads):
+            for b in range(n):
+                slot = pre_out.at[seq_source(b), head_source(k)]
+                remote(
+                    slot, slot, send_fan.at[b, k], recv_fan.at[b, k], {"head": head_peer(k)}
+                ).wait_recv()
+        loads[1].wait()
+        step = stored_rows
+
+        @pl.loop(0, total_rows // step)
+        def _(t):
+            at = pl.ds(pl.multiple_of(t * step, step), step)
+            order = order_ref[at, :]
+            lane = lax.broadcasted_iota(jnp.int32, (step, 128), 1)
+            wanted = jnp.where(
+                lane < n * tiles, lane // tiles * stored_rows + lane % tiles, -1
+            )
+            fresh_pick[at, :] = jnp.where(order == wanted, 1.0, 0.0).astype(jnp.bfloat16)
+            index = lax.broadcasted_iota(jnp.int32, (step, stored_rows), 1)
+            picks = [
+                jnp.where(order == index + b * stored_rows, 1.0, 0.0).astype(jnp.bfloat16)
+                for b in range(n)
+            ]
+            pieces = []
+            for j in range(heads):
+                piece = sum(
+                    jnp.dot(picks[b], pre_out[b, j], preferred_element_type=jnp.float32)
+                    for b in range(n)
+                )
+                seq_rows[j, at, :] = piece.astype(jnp.bfloat16)
+                pieces.append(piece)
+            normal = row_norm(pieces)
+            for g in range(3):
+                projected[g, at, :] = project(normal, g).astype(jnp.bfloat16)
+
     for d in range(1, n):
         relay(d)
         if d > 1:
             finish(d - 1)
+        if d == n - 1:
+            stored_sequence()
     if n > 1:
         finish(n - 1)
 
@@ -542,6 +641,8 @@
             remote(
                 slot, slot, send_seq.at[which, k], recv_seq.at[which, k], {"seq": seq_peer(k)}
             ).wait_recv()
+    loads[2].wait()
+    loads[3].wait()
     everyone = jnp.concatenate([pooled[b] for b in range(n)], axis=0)
     high = everyone.astype(jnp.bfloat16)
     rest = everyone - high.astype(jnp.float32)
@@ -578,8 +679,8 @@
         [sum(parts[b, j] for j in range(heads)) for b in range(n)], axis=1
     )
     average = jnp.concatenate([means[b] for b in range(n)], axis=0)
-    feature = normalize(average + scale_ref[...] * summed, fc_ref[...]).astype(jnp.bfloat16)
-    fresh = jnp.dot(feature, embed_ref[...], preferred_element_type=jnp.float32) + bias_ref[...]
+    feature = normalize(average + wide_ref[pl.ds(1, 1), :] * summed, wide_ref[pl.ds(2, 1), :]).astype(jnp.bfloat16)
+    fresh = jnp.dot(feature, embed_ref[...], preferred_element_type=jnp.float32) + narrow_ref[pl.ds(0, 1), :]
     new_out[hd] = fresh
     for k in range(1, heads):
         start(
@@ -596,146 +697,152 @@
             (sub_out.at[source], send_aux.at[1, k], recv_aux.at[1, k]),
         ):
             remote(slot, slot, sends, receives, peer).wait_recv()
-        for b in range(n):
-            slot = pre_out.at[seq_source(b), source]
-            remote(slot, slot, send_fan.at[b, k], recv_fan.at[b, k], peer).wait_recv()
+
+    pieces = [new_out[j].astype(jnp.bfloat16).astype(jnp.float32) for j in range(heads)]
+    normal = row_norm(pieces)
+    fresh_rows[...] = jnp.zeros(fresh_rows.shape, jnp.float32)
+    filled = pl.ds(0, n * tiles)
+    for g in range(3):
+        fresh_rows[g, filled, :] = project(normal, g)
+    fresh_rows[3, filled, :] = new_out[hd]
+    own_at = pl.ds(pl.multiple_of(z * own_rows, own_rows), own_rows)
+    updated = []
+    for g in range(3):
+        placed = jnp.dot(
+            fresh_pick[...],
+            fresh_rows[g].astype(jnp.bfloat16),
+            preferred_element_type=jnp.float32,
+        )
+        projected[g] = (projected[g].astype(jnp.float32) + placed).astype(jnp.bfloat16)
+    seq_rows[hd] = (
+        seq_rows[hd].astype(jnp.float32)
+        + jnp.dot(
+            fresh_pick[...],
+            fresh_rows[3].astype(jnp.bfloat16),
+            preferred_element_type=jnp.float32,
+        )
+    ).astype(jnp.bfloat16)
+
+    def class_part(buffer, lead, c):
+        return buffer[lead, pl.ds(pl.multiple_of(c * class_rows, class_rows), class_rows), :]
+
+    for c in range(classes):
+        at = pl.ds(
+            pl.multiple_of(c * class_rows + z * own_rows, own_rows), own_rows
+        )
+        own_query[c] = projected[0, at, :]
+        out_ref[pl.ds(c * own_rows, own_rows), :] = seq_rows[hd, at, :].astype(jnp.float32)
+
+    limit = valid_ref[0]
+    head_count = cols // HEAD_DIM
+    lane_head = lax.broadcasted_iota(jnp.int32, (1, cols), 1) // HEAD_DIM
+    factor = 1.0 / math.sqrt(HEAD_DIM)
+
+    def weigh(queries, keys, values, positions):
+        scores = (
+            lax.dot_general(
+                queries, keys, (((1,), (1,)), ((), ())), preferred_element_type=jnp.float32
+            )
+            * factor
+        )
+        scores = jnp.where(positions < limit, scores, masked_score)
+        peak = jnp.max(scores, axis=1, keepdims=True)
+        exponent = jnp.exp(scores - peak)
+        mass = jnp.sum(exponent, axis=1, keepdims=True)
+        weights = (exponent * (1.0 / mass)).astype(jnp.bfloat16)
+        return (
+            jnp.dot(weights, values, preferred_element_type=jnp.float32),
+            peak + jnp.log(mass),
+        )
+
+    block_size = classes * own_rows
+    row_index = lax.broadcasted_iota(jnp.int32, (block_size, 1), 0)
+    row_class = row_index // own_rows
+    row_position = z * block_size + row_index % own_rows * classes + row_class
+    near_lane = lax.broadcasted_iota(jnp.int32, (1, total_rows), 1)
+    near_position = near_lane % class_rows * classes + near_lane // class_rows
+    repeat = classes // DILATION_SECOND
+    mid_lane = lax.broadcasted_iota(jnp.int32, (1, repeat * class_rows), 1)
+    far_lane = lax.broadcasted_iota(jnp.int32, (1, class_rows), 1)
+    mid_out[...] = jnp.zeros(mid_out.shape, jnp.float32)
+    mid_mass[...] = jnp.zeros(mid_mass.shape, jnp.float32)
+    far_out[...] = jnp.zeros(far_out.shape, jnp.float32)
+    far_mass[...] = jnp.zeros(far_mass.shape, jnp.float32)
+    all_queries = own_query[...].reshape(block_size, cols)
+    nothing = jnp.zeros((), jnp.bfloat16)
+    combined = jnp.zeros((block_size, cols), jnp.float32)
+    for j in range(head_count):
+        here = lane_head == j
+        mid_offset = lax.rem(hd * head_count + j, DILATION_SECOND)
+        far_offset = lax.rem(hd * head_count + j, DILATION_THIRD)
+        near, near_log = weigh(
+            jnp.where(here, all_queries, nothing), projected[1], projected[2], near_position
+        )
+        mids = [mid_offset + DILATION_SECOND * t for t in range(repeat)]
+        mid, mid_log = weigh(
+            jnp.where(here, jnp.concatenate([own_query[c] for c in mids], axis=0), nothing),
+            jnp.concatenate([class_part(projected, 1, c) for c in mids], axis=0),
+            jnp.concatenate([class_part(projected, 2, c) for c in mids], axis=0),
+            mid_lane % class_rows * classes
+            + mid_lane // class_rows * DILATION_SECOND
+            + mid_offset,
+        )
+        far, far_log = weigh(
+            jnp.where(here, own_query[far_offset], nothing),
+            class_part(projected, 1, far_offset),
+            class_part(projected, 2, far_offset),
+            far_lane * classes + far_offset,
+        )
+        for t, c in enumerate(mids):
+            mid_out[j, c] = mid[t * own_rows : (t + 1) * own_rows]
+            mid_mass[j, c] = jnp.broadcast_to(
+                mid_log[t * own_rows : (t + 1) * own_rows], (own_rows, 128)
+            )
+        far_out[j, far_offset] = far
+        far_mass[j, far_offset] = jnp.broadcast_to(far_log, (own_rows, 128))
+        mid_log = mid_mass[j].reshape(block_size, 128)[:, :1]
+        far_log = far_mass[j].reshape(block_size, 128)[:, :1]
+        mid_used = row_class % DILATION_SECOND == mid_offset
+        far_used = row_class == far_offset
+        ceiling = jnp.maximum(near_log, jnp.where(mid_used, mid_log, near_log))
+        ceiling = jnp.maximum(ceiling, jnp.where(far_used, far_log, near_log))
+        near_share = jnp.exp(near_log - ceiling)
+        mid_share = jnp.where(mid_used, jnp.exp(mid_log - ceiling), 0.0)
+        far_share = jnp.where(far_used, jnp.exp(far_log - ceiling), 0.0)
+        mixture = (
+            near_share * near
+            + mid_share * mid_out[j].reshape(block_size, cols)
+            + far_share * far_out[j].reshape(block_size, cols)
+        ) / (near_share + mid_share + far_share)
+        combined = jnp.where(here, mixture, combined)
+    combined = jnp.where(row_position < limit, combined, 0.0)
+
+    slots[hd] = combined.astype(jnp.bfloat16)
+    for k in range(1, heads):
+        start(
+            remote(
+                slots.at[hd], slots.at[hd], send_mix.at[k], recv_mix.at[k], {"head": head_peer(k)}
+            )
+        )
+    for k in range(1, heads):
+        slot = slots.at[head_source(k)]
+        remote(slot, slot, send_mix.at[k], recv_mix.at[k], {"head": head_peer(k)}).wait_recv()
+    pieces = [slots[j].astype(jnp.float32) for j in range(heads)]
+    features = heads * cols
+    mean = sum(jnp.sum(p, axis=1, keepdims=True) for p in pieces) / features
+    square = sum(jnp.sum(p * p, axis=1, keepdims=True) for p in pieces) / features
+    scaling = lax.rsqrt(square - mean * mean + layer_eps)
+    branch = jnp.zeros(out_ref.shape, jnp.float32)
+    for j in range(heads):
+        gain = sub_out[j][1:2]
+        settled = ((pieces[j] - mean) * scaling * gain).astype(jnp.bfloat16)
+        branch += jnp.dot(settled, wcol_out[j], preferred_element_type=jnp.float32)
+    out_ref[...] += branch
     for copy, cond in pending:
         if cond is None:
             copy.wait_send()
         else:
             pl.when(cond)(copy.wait_send)
-
-
-def encode(
-    tile_tokens,
-    tile_gain,
-    w_gate_up,
-    w_down,
-    layer_scale,
-    fc_gain,
-    w_embed,
-    embed_bias,
-    pre_emb,
-    w_cols,
-    sub_gain,
-):
-    n = lax.axis_size("seq")
-    heads = lax.axis_size("head")
-    tiles, patch, width = tile_tokens.shape
-    depth, hidden_width = w_gate_up.shape[1:]
-    rows = tiles * patch
-    cols = w_embed.shape[1]
-    vmem = pl.BlockSpec(memory_space=pltpu.VMEM)
-    dma = pltpu.SemaphoreType.DMA
-    hops = max(n - 1, 1)
-    return pl.pallas_call(
-        functools.partial(encode_kernel, tiles),
-        out_shape=(
-            jax.ShapeDtypeStruct((n, heads) + pre_emb.shape, jnp.bfloat16),
-            jax.ShapeDtypeStruct((heads, n * tiles, cols), jnp.float32),
-            jax.ShapeDtypeStruct(w_cols.shape, jnp.bfloat16),
-            jax.ShapeDtypeStruct((heads, 1, cols), jnp.float32),
-        ),
-        in_specs=[vmem] * 11,
-        out_specs=(vmem,) * 4,
-        scratch_shapes=[
-            pltpu.VMEM((n, W_CHUNKS, 2 * depth // W_CHUNKS, hidden_width), jnp.bfloat16),
-            pltpu.VMEM((n, rows, depth), jnp.bfloat16),
-            pltpu.VMEM((2, rows, hidden_width), jnp.float32),
-            pltpu.VMEM((n, tiles, hidden_width), jnp.float32),
-            pltpu.VMEM((n, tiles, width), jnp.float32),
-            pltpu.VMEM((n, heads, n * tiles, w_down.shape[1]), jnp.float32),
-            dma((2, hops, W_CHUNKS)),
-            dma((2, hops, W_CHUNKS)),
-            dma((2, hops, W_CHUNKS)),
-            dma((2, hops, W_CHUNKS)),
-            dma((n,)),
-            dma((n,)),
-            dma((n, heads)),
-            dma((n, heads)),
-            dma((2, heads)),
-            dma((2, heads)),
-            dma((2, n)),
-            dma((2, n)),
-            dma((n, heads)),
-            dma((n, heads)),
-            dma((heads,)),
-            dma((heads,)),
-        ],
-        compiler_params=pltpu.CompilerParams(
-            collective_id=0, has_side_effects=True, vmem_limit_bytes=48 * 1024 * 1024
-        ),
-    )(
-        tile_tokens.reshape(rows, width),
-        tile_gain.reshape(1, width),
-        w_gate_up.reshape(W_CHUNKS, 2 * depth // W_CHUNKS, hidden_width),
-        w_down,
-        layer_scale.reshape(1, width),
-        fc_gain.reshape(1, width),
-        w_embed,
-        embed_bias.reshape(1, cols),
-        pre_emb,
-        w_cols,
-        sub_gain.reshape(1, cols),
-    )
-
-
-def settle_kernel(comb_ref, wcol_ref, sub_ref, out_ref, slots, send_sem, recv_sem):
-    heads = lax.axis_size("head")
-    hd = lax.axis_index("head")
-    barrier = pltpu.get_barrier_semaphore()
-    for k in range(1, heads):
-        pl.semaphore_signal(
-            barrier, inc=1, device_id={"head": lax.rem(hd + k, heads)}, device_id_type=MESH
-        )
-    pl.semaphore_wait(barrier, heads - 1)
-    copies = []
-    for k in range(1, heads):
-        copies.append(
-            remote(
-                comb_ref,
-                slots.at[hd],
-                send_sem.at[k],
-                recv_sem.at[k],
-                {"head": lax.rem(hd + k, heads)},
-            )
-        )
-        copies[-1].start()
-    slots[hd] = comb_ref[...]
-    for k in range(1, heads):
-        slot = slots.at[lax.rem(hd + heads - k, heads)]
-        remote(
-            slot, slot, send_sem.at[k], recv_sem.at[k], {"head": lax.rem(hd + k, heads)}
-        ).wait_recv()
-    pieces = [slots[j].astype(jnp.float32) for j in range(heads)]
-    features = heads * pieces[0].shape[1]
-    mean = sum(jnp.sum(p, axis=1, keepdims=True) for p in pieces) / features
-    square = sum(jnp.sum(p * p, axis=1, keepdims=True) for p in pieces) / features
-    scaling = lax.rsqrt(square - mean * mean + layer_eps)
-    total = jnp.zeros(out_ref.shape, jnp.float32)
-    for j in range(heads):
-        settled = ((pieces[j] - mean) * scaling * sub_ref[j]).astype(jnp.bfloat16)
-        total += jnp.dot(settled, wcol_ref[j], preferred_element_type=jnp.float32)
-    out_ref[...] = total
-    for copy in copies:
-        copy.wait_send()
-
-
-def settle(combined, w_cols, sub_all):
-    heads = lax.axis_size("head")
-    vmem = pl.BlockSpec(memory_space=pltpu.VMEM)
-    return pl.pallas_call(
-        settle_kernel,
-        out_shape=jax.ShapeDtypeStruct((combined.shape[0], w_cols.shape[2]), jnp.float32),
-        in_specs=[vmem] * 3,
-        out_specs=vmem,
-        scratch_shapes=[
-            pltpu.VMEM((heads,) + combined.shape, jnp.bfloat16),
-            pltpu.SemaphoreType.DMA((heads,)),
-            pltpu.SemaphoreType.DMA((heads,)),
-        ],
-        compiler_params=pltpu.CompilerParams(collective_id=1, has_side_effects=True),
-    )(combined, w_cols, sub_all)
 
 
 def near_body(
@@ -757,73 +864,103 @@
 ):
     n = lax.axis_size("seq")
     heads = lax.axis_size("head")
-    device = lax.axis_index("seq")
-    column = lax.axis_index("head")
+    tiles, patch, width = tile_tokens.shape
+    depth, hidden_width = w_gate_up.shape[1:]
+    rows = tiles * patch
     cols = w_embed.shape[1]
-    w_cols = w_out.reshape(cols, heads, cols).transpose(1, 0, 2)
-    pre_all, new_all, w_cols, sub_all = encode(
-        tile_tokens,
-        tile_gain,
-        w_gate_up,
-        w_down,
-        layer_scale,
-        fc_gain,
-        w_embed,
-        embed_bias,
-        pre_emb,
-        w_cols,
-        sub_gain,
-    )
+    head_count = cols // HEAD_DIM
     total_rows = tile_order.shape[0]
     block_rows = total_rows // n
-    new_rows = new_all.astype(jnp.bfloat16).transpose(1, 0, 2).reshape(n, -1, heads * cols)
-    old_rows = pre_all.transpose(0, 2, 1, 3).reshape(n, -1, heads * cols)
-    stored = jnp.concatenate([new_rows, old_rows], axis=1).reshape(total_rows, heads * cols)
-    every = jnp.arange(total_rows, dtype=jnp.int32)
-    routing = (tile_order[:, None] == every[None, :]).astype(jnp.bfloat16)
-    sequence = jnp.dot(routing, stored, preferred_element_type=jnp.float32)
-    slide_normed = normalize(sequence, slide_gain).astype(jnp.bfloat16)
-    key_value = jnp.einsum(
-        "rd,gdc->grc", slide_normed, w_qkv[1:], preferred_element_type=jnp.float32
-    ).astype(jnp.bfloat16)
-    own_normed = lax.dynamic_slice_in_dim(slide_normed, device * block_rows, block_rows)
-    query = jnp.dot(own_normed, w_qkv[0], preferred_element_type=jnp.float32).astype(jnp.bfloat16)
-    own_part = lax.dynamic_slice(
-        sequence, (device * block_rows, column * cols), (block_rows, cols)
-    )
-    head_count = cols // HEAD_DIM
-    head_indices = column * head_count + jnp.arange(head_count, dtype=jnp.int32)
-    valid_limit = valid_count[0]
-    row_index = device * block_rows + jnp.arange(block_rows, dtype=jnp.int32)
-    levels = []
-    for dilation in (1, DILATION_SECOND, DILATION_THIRD):
-        if dilation == 1:
-            positions = jnp.broadcast_to(every, (head_count, total_rows))
-            out, mass = attend(
-                query, key_value[0], key_value[1], positions, valid_limit, head_count
-            )
-            levels.append((out, mass, jnp.ones((block_rows, head_count), dtype=bool)))
-            continue
-        offsets = head_indices % dilation
-        chosen_query = select_rows(query[None], dilation, offsets)[0]
-        chosen = select_rows(key_value, dilation, offsets)
-        positions = (
-            offsets[:, None]
-            + dilation * jnp.arange(total_rows // dilation, dtype=jnp.int32)[None, :]
-        )
-        out, mass = attend(
-            chosen_query, chosen[0], chosen[1], positions, valid_limit, head_count
-        )
-        levels.append(scatter_rows(out, mass, dilation, offsets))
-    outputs, masses, selects = (jnp.stack(parts) for parts in zip(*levels))
-    ceiling = jnp.max(masses, axis=0)
-    shares = jnp.where(selects, jnp.exp(masses - ceiling), 0.0)
-    combined = jnp.sum(shares[..., None] * outputs, axis=0) / jnp.sum(shares, axis=0)[..., None]
-    combined = jnp.where((row_index < valid_limit)[:, None, None], combined, 0.0).reshape(
-        block_rows, cols
-    )
-    branch = settle(combined.astype(jnp.bfloat16), w_cols, sub_all)
-    return own_part + branch
+    classes = DILATION_THIRD
+    own_rows = block_rows // classes
+    w_cols = w_out.reshape(cols, heads, cols).transpose(1, 0, 2)
+    by_class = tile_order.reshape(total_rows // classes, classes).T.reshape(total_rows, 1)
+    vmem = pl.BlockSpec(memory_space=pltpu.VMEM)
+    anywhere = pl.BlockSpec(memory_space=pl.ANY)
+    dma = pltpu.SemaphoreType.DMA
+    hops = max(n - 1, 1)
+    f32, bf16 = jnp.float32, jnp.bfloat16
+    out = pl.pallas_call(
+        functools.partial(encode_kernel, tiles),
+        out_shape=jax.ShapeDtypeStruct((block_rows, cols), f32),
+        in_specs=[
+            pl.BlockSpec(memory_space=pltpu.SMEM),
+            anywhere,
+            vmem,
+            vmem,
+            anywhere,
+            anywhere,
+            vmem,
+            vmem,
+            vmem,
+            vmem,
+            vmem,
+            anywhere,
+        ],
+        out_specs=vmem,
+        scratch_shapes=[
+            pltpu.VMEM((rows, width), bf16),
+            pltpu.VMEM(w_down.shape, bf16),
+            pltpu.VMEM(w_embed.shape, bf16),
+            pltpu.VMEM(w_qkv.shape, bf16),
+            pltpu.VMEM((n, heads, block_rows, cols), bf16),
+            pltpu.VMEM((heads, n * tiles, cols), f32),
+            pltpu.VMEM(w_cols.shape, bf16),
+            pltpu.VMEM((heads, 2, cols), f32),
+            pltpu.VMEM((heads, total_rows, cols), bf16),
+            pltpu.VMEM((3, total_rows, cols), bf16),
+            pltpu.VMEM((total_rows, 128), bf16),
+            pltpu.VMEM((4, 128, cols), f32),
+            pltpu.VMEM((classes, own_rows, cols), bf16),
+            pltpu.VMEM((head_count, classes, own_rows, cols), f32),
+            pltpu.VMEM((head_count, classes, own_rows, 128), f32),
+            pltpu.VMEM((head_count, classes, own_rows, cols), f32),
+            pltpu.VMEM((head_count, classes, own_rows, 128), f32),
+            pltpu.VMEM((heads, block_rows, cols), bf16),
+            dma((4,)),
+            dma((heads,)),
+            dma((heads,)),
+            pltpu.VMEM((n, W_CHUNKS, 2 * depth // W_CHUNKS, hidden_width), bf16),
+            pltpu.VMEM((n, rows, depth), bf16),
+            pltpu.VMEM((2, rows, hidden_width), f32),
+            pltpu.VMEM((n, tiles, hidden_width), f32),
+            pltpu.VMEM((n, tiles, width), f32),
+            pltpu.VMEM((n, heads, n * tiles, w_down.shape[1]), f32),
+            dma((2, hops, W_CHUNKS)),
+            dma((2, hops, W_CHUNKS)),
+            dma((2, hops, W_CHUNKS)),
+            dma((2, hops, W_CHUNKS)),
+            dma((n,)),
+            dma((n,)),
+            dma((n, heads)),
+            dma((n, heads)),
+            dma((2, heads)),
+            dma((2, heads)),
+            dma((2, n)),
+            dma((2, n)),
+            dma((n, heads)),
+            dma((n, heads)),
+            dma((heads,)),
+            dma((heads,)),
+        ],
+        compiler_params=pltpu.CompilerParams(
+            collective_id=0, has_side_effects=True, vmem_limit_bytes=58 * 1024 * 1024
+        ),
+    )(
+        valid_count,
+        tile_tokens.reshape(rows, width),
+        jnp.stack([tile_gain, layer_scale, fc_gain]),
+        w_gate_up.reshape(W_CHUNKS, 2 * depth // W_CHUNKS, hidden_width),
+        w_down,
+        w_embed,
+        jnp.pad(pre_emb, ((tiles, 0), (0, 0))),
+        w_cols,
+        jnp.stack([embed_bias, sub_gain]),
+        by_class,
+        slide_gain.reshape(heads, cols),
+        w_qkv,
+    )
+    return out.reshape(classes, own_rows, cols).transpose(1, 0, 2).reshape(block_rows, cols)
 
 
 def body(*args):

time: 166 us -> 131 us (0.79)
  local copies, waits for them, and re-layouts: 29.1 us -> 14 us
  other arithmetic: 16.9 us -> 1.9 us
  matrix products: 6.78 us -> 0 us
  Pallas kernels: 111 us -> 114 us
    reduce_sum x10 -> x0, other arithmetic: 8.2 us -> none  [the longest x4 6.27 us: select_rows(): jnp.sum(jnp.where(choose[None, None, :, :, None], arranged, jnp.zeros((),...]
    unnamed x67 -> x7, local copies, waits for them, and re-layouts: 10.3 us -> 3.64 us
    dot_general x8 -> x0, matrix products: 6 us -> none  [the longest x1 2.06 us: near_body(): sequence = jnp.dot(routing, stored, preferred_element_type=jnp.float32)]
    pallas_call x2 -> x1, Pallas kernels: 111 us -> 114 us  [near_body(): pl.pallas_call(functools.partial(encode_kernel, tiles), out_shape=jax.Sha...]
    transpose x3 -> x1, local copies, waits for them, and re-layouts: 2.86 us -> 0.06 us  [near_body(): tile_order.reshape(total_rows // classes, classes).T.reshape(total_rows, 1)]
    broadcast_in_dim x14 -> x0, local copies, waits for them, and re-layouts: 2.47 us -> none  [the longest x4 1.38 us: scatter_rows(): jnp.broadcast_to(choose[None, :, :], (query_count, dilation, head_count))]
    lt x4 -> x0, other arithmetic: 2.42 us -> none  [the longest x3 1.83 us: attend(): positions < valid_limit]
    select_n x5 -> x0, other arithmetic: 2.05 us -> none  [the longest x2 1.36 us: scatter_rows(): jnp.where(choose[None, :, :, None], attended[:, None, :, :], 0.0)]
where the time goes in v2:
time: 131 us
  Pallas kernels  114 us (87%)
  local copies, waits for them, and re-layouts  14 us (11%)
  other arithmetic  1.9 us (1%)
    pallas_call x1, Pallas kernels, near_body(): pl.pallas_call(functools.partial(encode_kernel, tiles), out_shape=jax.Sha...  114 us
    unnamed x7, local copies, waits for them, and re-layouts  3.64 us

profile of v2, /device:TPU:1, one launch (start us, length us, event | category | flops | bytes accessed | tf_op | source)
XLA Modules:
  0.0 130.6 jit_solution(11618108767802010006)
XLA Ops:
  0.0 0.0 copy-start.1
  0.7 1.3 pad_maximum_fusion.1.narrow_ref
  2.0 1.4 %reshape.29.slide_ref = f32[4,192]{1,0:T(4,128)} reshape(f32[768]{0:T(1024)} %param.26) | data formatting | bytes 6144 | tf_op jit(solution)/shard_map/reshape | solution.py:960
  3.3 0.7 stack.21
  4.0 0.7 stack.22
  4.8 0.7 stack.23
  5.5 0.6 pad_maximum_fusion.wide_ref
  6.1 0.8 reshape.27
  6.8 0.1 copy.22
  6.9 1.0 copy.20
  7.9 0.7 pad.4.pre_ref
  8.6 0.0 copy-start
  8.6 1.4 %reshape.26 = bf16[192,4,192]{2,1,0:T(4,128)(2,1)S(1)} reshape(bf16[192,768]{1,0:T(8,128)(2,1)} %param.29) | data formatting | bytes 589824 | tf_op jit(solution)/shard_map/reshape | solution.py:876
  10.0 0.8 copy.29
  10.8 1.3 reshape.32.order_ref
  12.1 0.0 copy-done.1
  12.1 1.2 copy.23.embed_hbm
  13.3 0.0 copy-done
  13.3 1.4 %copy.25.qkv_hbm = bf16[3,768,192]{2,1,0:T(8,128)(2,1)} copy(bf16[3,768,192]{1,2,0:T(8,128)(2,1)S(1)} %copy-done) | data formatting | bytes 1769472 | tf_op args[12]
  14.7 113.9 %shard_map.145 = f32[256,192]{1,0:T(8,128)} custom-call(s32[1]{0:T(128)S(6)} %copy.30.valid_ref, bf16[512,1536]{1,0:T(8,128)(2,1)} %bitcast.13, f32[3,1536]{1,0:T(4,128)} %pad_maximum_fusion.wide_ref, bf16[8,96,1024]{2,1,0:T(8,128)(2,1)} %bitcast.14, bf16[1024,384]{1,0:T(8,128)(2,1)} %down_hbm.1, bf16[1536,192]{1,0:T(8,128)(2,1)} %copy.23.embed_hbm, ...), custom_call_target="tpu_custom_call" | custom-call | tf_op jit(solution)/shard_map/pallas_call | solution.py:883
  128.7 1.1 copy.26
  129.8 0.8 copy.27
Async XLA Ops:
  0.0 12.1 %copy-start.1 = (bf16[1536,192]{0,1:T(8,128)(2,1)S(1)}, bf16[1536,192]{0,1:T(8,128)(2,1)}, u32[]{:S(2)}) copy-start(bf16[1536,192]{0,1:T(8,128)(2,1)} %param.21) | copy-start | bytes 1769476
  8.6 4.7 %copy-start = (bf16[3,768,192]{1,2,0:T(8,128)(2,1)S(1)}, bf16[3,768,192]{1,2,0:T(8,128)(2,1)}, u32[]{:S(2)}) copy-start(bf16[3,768,192]{1,2,0:T(8,128)(2,1)} %param.27) | copy-start | bytes 2654212

commit v3 on v2

--- a/solution.py
+++ b/solution.py
@@ -250,11 +250,19 @@
     )
 
 
+def dot_rows(left, right):
+    return lax.dot_general(
+        left, right, (((1,), (1,)), ((), ())), preferred_element_type=jnp.float32
+    )
+
+
 def encode_kernel(
     tiles,
     valid_ref,
     tok_hbm,
-    wide_ref,
+    gain_ref,
+    scale_ref,
+    fc_ref,
     w_ref,
     down_hbm,
     embed_hbm,
@@ -269,6 +277,8 @@
     down_ref,
     embed_ref,
     qkv_ref,
+    qkv_parts,
+    wcol_parts,
     pre_out,
     new_out,
     wcol_out,
@@ -284,6 +294,8 @@
     far_mass,
     slots,
     local_sem,
+    send_tok,
+    recv_tok,
     send_mix,
     recv_mix,
     wall,
@@ -315,11 +327,13 @@
     z = lax.axis_index("seq")
     hd = lax.axis_index("head")
     y = lax.axis_index("groups")
-    rows, width = tok_ref.shape
+    rows, width = tok_hbm.shape
     patch = rows // tiles
     depth = width // n
     hidden_width = w_ref.shape[2]
     half = W_CHUNKS // 2
+    narrow = wcol_ref.shape[0]
+    half_width = hidden_width // 2
 
     def seq_peer(k):
         return lax.rem(z + k, n)
@@ -349,7 +363,7 @@
         pltpu.make_async_copy(source, target, local_sem.at[i])
         for i, (source, target) in enumerate(
             (
-                (tok_hbm, tok_ref),
+                (tok_hbm, tok_ref.at[pl.ds(pl.multiple_of(lax.rem(z, 2) * rows, rows), rows)]),
                 (qkv_hbm, qkv_ref),
                 (down_hbm, down_ref),
                 (embed_hbm, embed_ref),
@@ -384,28 +398,56 @@
             pl.when(cond)(copy.start)
         pending.append((copy, cond))
 
-    for k in range(1, n):
-        start(
-            remote(
-                pre_ref, pre_out.at[z, hd], send_pre.at[k], recv_pre.at[k], {"seq": seq_peer(k)}
-            )
-        )
-    step_right = {"seq": lax.min(z + 1, n - 1)}
-    step_left = {"seq": lax.max(z - 1, 0)}
-    for i in range(carry):
-        c = chunk(y, i)
-        start(
-            remote(w_ref.at[c], wall.at[z, c], send_w.at[0, 0, i], recv_w.at[0, 0, i], step_right),
-            z + 1 < n,
-        )
-        start(
-            remote(w_ref.at[c], wall.at[z, c], send_w.at[1, 0, i], recv_w.at[1, 0, i], step_left),
-            z >= 1,
-        )
+    part = lax.rem(z, 2)
+    partner = z + 1 - 2 * part
+    quarter = rows // heads
+
+    def token_rows(member, share):
+        return pl.ds(pl.multiple_of(member * rows + share * quarter, quarter), quarter)
+
+    start(
+        remote(
+            tok_hbm.at[pl.ds(pl.multiple_of(hd * quarter, quarter), quarter)],
+            tok_ref.at[token_rows(part, hd)],
+            send_tok.at[0],
+            recv_tok.at[0],
+            {"seq": partner},
+        )
+    )
+    for d in range(1, n):
+        for i in range(carry):
+            c = chunk(y, i)
+            for side in range(2):
+                goes = z + d < n if side == 0 else z >= d
+                target = lax.min(z + d, n - 1) if side == 0 else lax.max(z - d, 0)
+                at = pl.ds(pl.multiple_of(lax.rem(target, 2) * half_width, half_width), half_width)
+                start(
+                    remote(
+                        w_ref.at[c, :, at],
+                        wall.at[z, c],
+                        send_w.at[side, d - 1, i],
+                        recv_w.at[side, d - 1, i],
+                        {"seq": target},
+                    ),
+                    goes,
+                )
+        if d == 1:
+            for k in range(1, n):
+                start(
+                    remote(
+                        pre_ref,
+                        pre_out.at[z, hd],
+                        send_pre.at[k],
+                        recv_pre.at[k],
+                        {"seq": seq_peer(k)},
+                    )
+                )
+    for j in range(heads):
+        wcol_parts[j] = wcol_ref[:, j * narrow : (j + 1) * narrow]
     for k in range(1, heads):
         start(
             remote(
-                wcol_ref.at[head_peer(k)],
+                wcol_parts.at[head_peer(k)],
                 wcol_out.at[hd],
                 send_aux.at[0, k],
                 recv_aux.at[0, k],
@@ -427,51 +469,68 @@
             )
         )
     pre_out[z, hd] = pre_ref[...]
-    wcol_out[hd] = wcol_ref[hd]
+    wcol_out[hd] = wcol_parts[hd]
     sub_out[hd] = narrow_ref[...]
 
     loads[0].wait()
     block = 64
-    means[z] = jnp.zeros((tiles, width), jnp.float32)
-    for tile in range(tiles):
-
-        def norm_rows(i, total):
-            at = pl.ds(pl.multiple_of(tile * patch + i * block, block), block)
-            values = tok_ref[at, :].astype(jnp.float32)
-            out = normalize(values, wide_ref[pl.ds(0, 1), :]).astype(jnp.bfloat16)
-            for b in range(n):
-                normed[b, at, :] = out[:, b * depth : (b + 1) * depth]
-            return total + jnp.sum(values, axis=0, keepdims=True)
-
-        total = lax.fori_loop(0, patch // block, norm_rows, jnp.zeros((1, width), jnp.float32))
-        means[z, pl.ds(tile, 1), :] = total / patch
+
+    def norm_tokens(member, keep_mean):
+        for tile in range(tiles):
+
+            def norm_rows(i, total):
+                at = pl.ds(
+                    pl.multiple_of(member * rows + tile * patch + i * block, block), block
+                )
+                values = tok_ref[at, :].astype(jnp.float32)
+                out = normalize(values, gain_ref[...].reshape(1, width)).astype(jnp.bfloat16)
+                for b in range(n):
+                    normed[b, at, :] = out[:, b * depth : (b + 1) * depth]
+                if keep_mean:
+                    total = total + jnp.sum(values, axis=0, keepdims=True)
+                return total
+
+            total = lax.fori_loop(
+                0, patch // block, norm_rows, jnp.zeros((1, width), jnp.float32)
+            )
+            if keep_mean:
+                means[z, pl.ds(tile, 1), :] = total / patch
+
+    norm_tokens(part, True)
     for k in range(1, n):
         start(
             remote(
                 means.at[z], means.at[z], send_seq.at[0, k], recv_seq.at[0, k], {"seq": seq_peer(k)}
             )
         )
+    slot = tok_ref.at[token_rows(1 - part, hd)]
+    remote(slot, slot, send_tok.at[0], recv_tok.at[0], {"seq": partner}).wait_recv()
+    for k in range(1, heads):
+        start(remote(slot, slot, send_tok.at[k], recv_tok.at[k], {"head": head_peer(k)}))
 
     columns = 256
 
     def multiply(weights, owner, first):
-        @pl.loop(0, hidden_width // columns)
+        @pl.loop(0, 2 * (half_width // columns))
         def _(t):
-            at = pl.ds(pl.multiple_of(t * columns, columns), columns)
+            member = lax.rem(t, 2)
+            at = pl.ds(pl.multiple_of(t // 2 * columns, columns), columns)
+            span = pl.ds(pl.multiple_of(member * rows, rows), rows)
             for g in range(2):
                 if owner is None:
-                    w = weights[pl.ds(g * half, half), :, at]
+                    place = part * half_width + t // 2 * columns
+                    w = weights[
+                        pl.ds(g * half, half), :, pl.ds(pl.multiple_of(place, columns), columns)
+                    ]
                 else:
                     w = weights[owner, pl.ds(g * half, half), :, at]
                 w = w.reshape(depth, columns)
-                x = normed[z if owner is None else owner]
+                x = normed[z if owner is None else owner, span, :]
                 value = jnp.dot(x, w, preferred_element_type=jnp.float32)
                 if first:
-                    acc[g, :, at] = value
+                    acc[g, span, at] = value
                 else:
-                    acc[g, :, at] += value
-
-    multiply(w_ref, None, True)
+                    acc[g, span, at] += value
 
     def owner_of(side, d):
         return lax.max(z - d, 0) if side == 0 else lax.min(z + d, n - 1)
@@ -486,17 +545,14 @@
                 o = owner_of(side, d)
                 slot = wall.at[o, c]
                 there = valid(side, d)
-                onward = step_right if side == 0 else step_left
                 arrive = remote(
-                    slot, slot, send_w.at[side, d - 1, i], recv_w.at[side, d - 1, i], onward
+                    slot,
+                    slot,
+                    send_w.at[side, d - 1, i],
+                    recv_w.at[side, d - 1, i],
+                    {"seq": o},
                 )
                 pl.when(there)(arrive.wait_recv)
-                if d + 1 < n:
-                    goes = (z + 1 < n) if side == 0 else (z >= 1)
-                    start(
-                        remote(slot, slot, send_w.at[side, d, i], recv_w.at[side, d, i], onward),
-                        there & goes,
-                    )
                 if i < swap:
                     start(
                         remote(
@@ -539,10 +595,8 @@
                     )
                 )
 
-    fan_out()
     total_rows = order_ref.shape[0]
-    stored_rows = pre_ref.shape[0]
-    cols = pre_ref.shape[1]
+    cols, stored_rows = pre_ref.shape
     classes = DILATION_THIRD
     class_rows = total_rows // classes
     own_rows = stored_rows // classes
@@ -560,11 +614,7 @@
 
     def project(pieces, g):
         return sum(
-            jnp.dot(
-                piece,
-                qkv_ref[g, j * cols : (j + 1) * cols, :],
-                preferred_element_type=jnp.float32,
-            )
+            dot_rows(piece, qkv_parts[g, j])
             for j, piece in enumerate(pieces)
         )
 
@@ -576,6 +626,9 @@
                     slot, slot, send_fan.at[b, k], recv_fan.at[b, k], {"head": head_peer(k)}
                 ).wait_recv()
         loads[1].wait()
+        for g in range(3):
+            for j in range(heads):
+                qkv_parts[g, j] = qkv_ref[g, :, j * cols : (j + 1) * cols]
         step = stored_rows
 
         @pl.loop(0, total_rows // step)
@@ -595,7 +648,7 @@
             pieces = []
             for j in range(heads):
                 piece = sum(
-                    jnp.dot(picks[b], pre_out[b, j], preferred_element_type=jnp.float32)
+                    dot_rows(picks[b], pre_out[b, j])
                     for b in range(n)
                 )
                 seq_rows[j, at, :] = piece.astype(jnp.bfloat16)
@@ -604,18 +657,25 @@
             for g in range(3):
                 projected[g, at, :] = project(normal, g).astype(jnp.bfloat16)
 
-    for d in range(1, n):
-        relay(d)
-        if d > 1:
-            finish(d - 1)
+    relay(1)
+    fan_out()
+    for k in range(1, heads):
+        slot = tok_ref.at[token_rows(1 - part, head_source(k))]
+        remote(slot, slot, send_tok.at[k], recv_tok.at[k], {"head": head_peer(k)}).wait_recv()
+    norm_tokens(1 - part, False)
+    multiply(w_ref, None, True)
+    for d in range(2, n):
         if d == n - 1:
             stored_sequence()
-    if n > 1:
-        finish(n - 1)
-
-    for tile in range(tiles):
-
-        @pl.loop(0, hidden_width // columns)
+        relay(d)
+        finish(d - 1)
+    if n == 2:
+        stored_sequence()
+    finish(n - 1)
+
+    for tile in range(2 * tiles):
+
+        @pl.loop(0, half_width // columns)
         def _(t):
             at = pl.ds(pl.multiple_of(t * columns, columns), columns)
             span = pl.ds(tile * patch, patch)
@@ -643,7 +703,9 @@
             ).wait_recv()
     loads[2].wait()
     loads[3].wait()
-    everyone = jnp.concatenate([pooled[b] for b in range(n)], axis=0)
+    everyone = jnp.concatenate(
+        [jnp.concatenate([pooled[b], pooled[b + 1]], axis=1) for b in range(0, n, 2)], axis=0
+    )
     high = everyone.astype(jnp.bfloat16)
     rest = everyone - high.astype(jnp.float32)
     middle = rest.astype(jnp.bfloat16)
@@ -679,8 +741,8 @@
         [sum(parts[b, j] for j in range(heads)) for b in range(n)], axis=1
     )
     average = jnp.concatenate([means[b] for b in range(n)], axis=0)
-    feature = normalize(average + wide_ref[pl.ds(1, 1), :] * summed, wide_ref[pl.ds(2, 1), :]).astype(jnp.bfloat16)
-    fresh = jnp.dot(feature, embed_ref[...], preferred_element_type=jnp.float32) + narrow_ref[pl.ds(0, 1), :]
+    feature = normalize(average + scale_ref[...].reshape(1, width) * summed, fc_ref[...].reshape(1, width)).astype(jnp.bfloat16)
+    fresh = dot_rows(feature, embed_ref[...]) + narrow_ref[pl.ds(0, 1), :]
     new_out[hd] = fresh
     for k in range(1, heads):
         start(
@@ -873,7 +935,6 @@
     block_rows = total_rows // n
     classes = DILATION_THIRD
     own_rows = block_rows // classes
-    w_cols = w_out.reshape(cols, heads, cols).transpose(1, 0, 2)
     by_class = tile_order.reshape(total_rows // classes, classes).T.reshape(total_rows, 1)
     vmem = pl.BlockSpec(memory_space=pltpu.VMEM)
     anywhere = pl.BlockSpec(memory_space=pl.ANY)
@@ -888,6 +949,8 @@
             anywhere,
             vmem,
             vmem,
+            vmem,
+            vmem,
             anywhere,
             anywhere,
             vmem,
@@ -899,13 +962,15 @@
         ],
         out_specs=vmem,
         scratch_shapes=[
-            pltpu.VMEM((rows, width), bf16),
+            pltpu.VMEM((2 * rows, width), bf16),
             pltpu.VMEM(w_down.shape, bf16),
-            pltpu.VMEM(w_embed.shape, bf16),
-            pltpu.VMEM(w_qkv.shape, bf16),
-            pltpu.VMEM((n, heads, block_rows, cols), bf16),
+            pltpu.VMEM((cols, width), bf16),
+            pltpu.VMEM((3, cols, heads * cols), bf16),
+            pltpu.VMEM((3, heads, cols, cols), bf16),
+            pltpu.VMEM((heads, cols, cols), bf16),
+            pltpu.VMEM((n, heads, cols, block_rows), bf16),
             pltpu.VMEM((heads, n * tiles, cols), f32),
-            pltpu.VMEM(w_cols.shape, bf16),
+            pltpu.VMEM((heads, cols, cols), bf16),
             pltpu.VMEM((heads, 2, cols), f32),
             pltpu.VMEM((heads, total_rows, cols), bf16),
             pltpu.VMEM((3, total_rows, cols), bf16),
@@ -920,10 +985,12 @@
             dma((4,)),
             dma((heads,)),
             dma((heads,)),
-            pltpu.VMEM((n, W_CHUNKS, 2 * depth // W_CHUNKS, hidden_width), bf16),
-            pltpu.VMEM((n, rows, depth), bf16),
-            pltpu.VMEM((2, rows, hidden_width), f32),
-            pltpu.VMEM((n, tiles, hidden_width), f32),
+            dma((heads,)),
+            dma((heads,)),
+            pltpu.VMEM((n, W_CHUNKS, 2 * depth // W_CHUNKS, hidden_width // 2), bf16),
+            pltpu.VMEM((n, 2 * rows, depth), bf16),
+            pltpu.VMEM((2, 2 * rows, hidden_width // 2), f32),
+            pltpu.VMEM((n, 2 * tiles, hidden_width // 2), f32),
             pltpu.VMEM((n, tiles, width), f32),
             pltpu.VMEM((n, heads, n * tiles, w_down.shape[1]), f32),
             dma((2, hops, W_CHUNKS)),
@@ -949,23 +1016,25 @@
     )(
         valid_count,
         tile_tokens.reshape(rows, width),
-        jnp.stack([tile_gain, layer_scale, fc_gain]),
+        tile_gain,
+        layer_scale,
+        fc_gain,
         w_gate_up.reshape(W_CHUNKS, 2 * depth // W_CHUNKS, hidden_width),
         w_down,
-        w_embed,
-        jnp.pad(pre_emb, ((tiles, 0), (0, 0))),
-        w_cols,
+        w_embed.T,
+        jnp.pad(pre_emb.T, ((0, 0), (tiles, 0))),
+        w_out,
         jnp.stack([embed_bias, sub_gain]),
         by_class,
         slide_gain.reshape(heads, cols),
-        w_qkv,
+        w_qkv.swapaxes(1, 2),
     )
     return out.reshape(classes, own_rows, cols).transpose(1, 0, 2).reshape(block_rows, cols)
 
 
 def body(*args):
     total_rows = args[9].shape[0]
-    if total_rows <= SPAN0:
+    if total_rows <= SPAN0 and lax.axis_size("seq") % 2 == 0:
         return near_body(*args)
     return general_body(*args)
 

time: 131 us -> 112 us (0.85)
  Pallas kernels: 114 us -> 103 us
  local copies, waits for them, and re-layouts: 14 us -> 6.98 us
    pallas_call x1, Pallas kernels: 114 us -> 103 us  [near_body(): pl.pallas_call(functools.partial(encode_kernel, tiles), out_shape=jax.Sha...]
    unnamed x7 -> x0, local copies, waits for them, and re-layouts: 3.64 us -> none
    reshape x2 -> x0, local copies, waits for them, and re-layouts: 2.22 us -> none  [near_body(): w_cols = w_out.reshape(cols, heads, cols).transpose(1, 0, 2)]
    another operation x3 -> x0, local copies, waits for them, and re-layouts: 2.1 us -> none  [near_body(): jnp.stack([tile_gain, layer_scale, fc_gain])]
where the time goes in v3:
time: 112 us; the launch traced here: 111 us
  Pallas kernels  103 us (92%)
  local copies, waits for them, and re-layouts  6.98 us (6%)
  other arithmetic  1.29 us (1%)
    pallas_call x1, Pallas kernels, near_body(): pl.pallas_call(functools.partial(encode_kernel, tiles), out_shape=jax.Sha...  103 us

profile of v3, /device:TPU:1, one launch (start us, length us, event | category | flops | bytes accessed | tf_op | source)
XLA Modules:
  0.0 111.5 jit_solution(4695746132427574956)
XLA Ops:
  0.7 1.3 %pad_maximum_fusion.narrow_ref = f32[2,192]{1,0:T(2,128)} fusion(f32[1,192]{1,0:T(1,128)} %bitcast.20, f32[1,192]{1,0:T(1,128)} %bitcast.21), kind=kLoop, calls=%fused_computation | loop fusion | flops 384 | bytes 3072 | tf_op jit(solution)/shard_map/stack | solution.py:1027
  1.9 1.4 %reshape.25.slide_ref = f32[4,192]{1,0:T(4,128)} reshape(f32[768]{0:T(1024)} %param.26) | data formatting | bytes 6144 | tf_op jit(solution)/shard_map/reshape | solution.py:1029
  3.3 0.8 reshape.23
  4.1 0.1 copy.17
  4.1 1.6 %pad.4.pre_ref = bf16[192,256]{1,0:T(8,128)(2,1)} pad(bf16[192,254]{1,0:T(8,128)(2,1)} %bitcast.19, bf16[]{:T(256)} %constant.2.clone.1), padding=0_0x2_0 | pad | bytes 195842 | tf_op jit(solution)/shard_map/jit(_pad)/pad | solution.py:1025
  5.8 1.3 %reshape.28.order_ref = s32[1024,1]{1,0:T(8,128)} reshape(s32[16,64]{1,0:T(8,128)S(1)} %copy.17) | data formatting | bytes 8192 | tf_op jit(solution)/shard_map/reshape | solution.py:938
  7.0 102.6 %shard_map.145 = f32[256,192]{1,0:T(8,128)} custom-call(s32[1]{0:T(128)S(6)} %copy.21.valid_ref, bf16[512,1536]{1,0:T(8,128)(2,1)} %bitcast.12, f32[1536]{0:T(1024)} %gain_ref.1, f32[1536]{0:T(1024)} %scale_ref.1, f32[1536]{0:T(1024)} %fc_ref.1, bf16[8,96,1024]{2,1,0:T(8,128)(2,1)} %bitcast.13, bf16[1024,384]{1,0:T(8,128)(2,1)} %down_hbm.1, ...), custom_call_target="tpu_custom_call" | custom-call | tf_op jit(solution)/shard_map/pallas_call | solution.py:944
  109.6 1.1 copy.19
  110.7 0.8 copy.20

commit v4 on v3

--- a/solution.py
+++ b/solution.py
@@ -268,7 +268,8 @@
     embed_hbm,
     pre_ref,
     wcol_ref,
-    narrow_ref,
+    bias_ref,
+    sub_ref,
     order_ref,
     slide_ref,
     qkv_hbm,
@@ -279,6 +280,7 @@
     qkv_ref,
     qkv_parts,
     wcol_parts,
+    narrow_ref,
     pre_out,
     new_out,
     wcol_out,
@@ -442,6 +444,8 @@
                         {"seq": seq_peer(k)},
                     )
                 )
+    narrow_ref[pl.ds(0, 1), :] = bias_ref[...].reshape(1, narrow)
+    narrow_ref[pl.ds(1, 1), :] = sub_ref[...].reshape(1, narrow)
     for j in range(heads):
         wcol_parts[j] = wcol_ref[:, j * narrow : (j + 1) * narrow]
     for k in range(1, heads):
@@ -608,7 +612,7 @@
         variance = sum(jnp.sum(p * p, axis=1, keepdims=True) for p in centered) / features
         scaling = lax.rsqrt(variance + layer_eps)
         return [
-            (p * scaling * slide_ref[pl.ds(j, 1), :]).astype(jnp.bfloat16)
+            (p * scaling * slide_ref[...].reshape(1, features)[:, j * cols : (j + 1) * cols]).astype(jnp.bfloat16)
             for j, p in enumerate(centered)
         ]
 
@@ -958,6 +962,7 @@
             vmem,
             vmem,
             vmem,
+            vmem,
             anywhere,
         ],
         out_specs=vmem,
@@ -968,6 +973,7 @@
             pltpu.VMEM((3, cols, heads * cols), bf16),
             pltpu.VMEM((3, heads, cols, cols), bf16),
             pltpu.VMEM((heads, cols, cols), bf16),
+            pltpu.VMEM((2, cols), f32),
             pltpu.VMEM((n, heads, cols, block_rows), bf16),
             pltpu.VMEM((heads, n * tiles, cols), f32),
             pltpu.VMEM((heads, cols, cols), bf16),
@@ -1024,9 +1030,10 @@
         w_embed.T,
         jnp.pad(pre_emb.T, ((0, 0), (tiles, 0))),
         w_out,
-        jnp.stack([embed_bias, sub_gain]),
+        embed_bias,
+        sub_gain,
         by_class,
-        slide_gain.reshape(heads, cols),
+        slide_gain,
         w_qkv.swapaxes(1, 2),
     )
     return out.reshape(classes, own_rows, cols).transpose(1, 0, 2).reshape(block_rows, cols)

time: 112 us -> 109 us (0.973)
  local copies, waits for them, and re-layouts: 6.98 us -> 5.63 us
  other arithmetic: 1.29 us -> 0 us
    reshape x1 -> x0, local copies, waits for them, and re-layouts: 1.35 us -> none  [near_body(): slide_gain.reshape(heads, cols)]
    another operation x1 -> x0, other arithmetic: 1.29 us -> none  [near_body(): jnp.stack([embed_bias, sub_gain])]
where the time goes in v4:
time: 109 us
  Pallas kernels  103 us (94%)
  local copies, waits for them, and re-layouts  5.63 us (5%)
    pallas_call x1, Pallas kernels, near_body(): pl.pallas_call(functools.partial(encode_kernel, tiles), out_shape=jax.Sha...  103 us

profile of v4, /device:TPU:1, one launch (start us, length us, event | category | flops | bytes accessed | tf_op | source)
XLA Modules:
  0.0 108.9 jit_solution(12789251719458788751)
XLA Ops:
  0.7 0.8 reshape.20
  1.4 0.1 copy.17
  1.5 1.6 %pad.4.pre_ref = bf16[192,256]{1,0:T(8,128)(2,1)} pad(bf16[192,254]{1,0:T(8,128)(2,1)} %bitcast.17, bf16[]{:T(256)} %constant.2.clone.1), padding=0_0x2_0 | pad | bytes 195842 | tf_op jit(solution)/shard_map/jit(_pad)/pad | solution.py:1031
  3.1 1.3 %reshape.24.order_ref = s32[1024,1]{1,0:T(8,128)} reshape(s32[16,64]{1,0:T(8,128)S(1)} %copy.17) | data formatting | bytes 8192 | tf_op jit(solution)/shard_map/reshape | solution.py:942
  4.4 102.6 %shard_map.145 = f32[256,192]{1,0:T(8,128)} custom-call(s32[1]{0:T(128)S(6)} %copy.21.valid_ref, bf16[512,1536]{1,0:T(8,128)(2,1)} %bitcast.10, f32[1536]{0:T(1024)} %gain_ref.1, f32[1536]{0:T(1024)} %scale_ref.1, f32[1536]{0:T(1024)} %fc_ref.1, bf16[8,96,1024]{2,1,0:T(8,128)(2,1)} %bitcast.11, bf16[1024,384]{1,0:T(8,128)(2,1)} %down_hbm.1, ...), custom_call_target="tpu_custom_call" | custom-call | tf_op jit(solution)/shard_map/pallas_call | solution.py:948
  107.0 1.1 %copy.19 = f32[16,16,192]{2,0,1:T(8,128)S(1)} copy(f32[16,16,192]{2,1,0:T(8,128)} %bitcast.12) | data formatting | bytes 393216 | tf_op jit(solution)/shard_map/reshape | solution.py:1039
  108.1 0.8 copy.20
